TPU v7x, 32 devices: a whole 2x2x4 slice. The times are simulated.
32 devices in a mesh: tri: 16 (over z, y, x), sub: 2 (over core).
Axes of the slice: x: 2, y: 2, z: 4, core: 2. Of those that a mesh axis runs over, the one named last changes fastest.
Arguments:
- stored_tiles: float32 [16, 36, 512, 512], P('tri', None, 'sub'), may hold values from -190 to 190, as said below
- cell_owner: int32 [16], replicated, may hold values from 0 to 15, as said below
Outputs:
- updated: float32 [16, 36, 512, 512], P('tri', None, 'sub')
Inputs may be any that keep to these rules, and one draw needn't show every extreme that they name: `cell_owner`: a permutation of the indices of tri. `stored_tiles`: every tile whose row and column blocks are equal is skew-symmetric, every pivot met is invertible, and slots that hold no tile are zero.
All inputs are finite; a program needn't handle non-finite values.
Results may differ from a plain program's by a relative error of at most 0.00035.
Values may be sent and summed in bfloat16 or wider, within the bound.
No kernel may reach another device: no remote copies, remote signals or barrier semaphores. Data moves between devices by JAX's collectives and lax.ppermute only.
A program may use at most 128 MiB of HBM per device.

v0:
```python
import math

import jax
import jax.numpy as jnp
import numpy as np
from jax import lax
from jax.experimental import pallas as pl
from jax.experimental.pallas import tpu as pltpu
from jax.sharding import PartitionSpec as P


NB = 32


def shortened(x):

    def short(part):
        return part.astype(jnp.bfloat16) if part.dtype == jnp.float32 else part

    return jax.tree.map(short, x)


def layout(groups, per_group):
    half_group = per_group // 2
    slot_count = per_group * (per_group + 1) // 2
    row_table = np.full((groups * groups, slot_count), -1, np.int32)
    col_table = np.full((groups * groups, slot_count), -1, np.int32)
    for first_group in range(groups):
        for second_group in range(groups):
            cell_index = first_group * groups + second_group
            for inner_row in range(per_group):
                if first_group == second_group:
                    for inner_column in range(inner_row + 1):
                        slot_index = inner_row * (inner_row + 1) // 2 + inner_column
                        row_table[cell_index, slot_index] = first_group * per_group + inner_row
                        col_table[cell_index, slot_index] = first_group * per_group + inner_column
                else:
                    for inner_column in range(half_group):
                        slot_index = inner_row * half_group + inner_column
                        if first_group > second_group:
                            row_table[cell_index, slot_index] = first_group * per_group + inner_row
                            col_table[cell_index, slot_index] = (
                                second_group * per_group + inner_column
                            )
                        else:
                            row_table[cell_index, slot_index] = second_group * per_group + inner_row
                            col_table[cell_index, slot_index] = (
                                first_group * per_group + half_group + inner_column
                            )
    return (row_table, col_table)


def untiled(stored_tiles, cell_owner):
    tri_count = lax.axis_size("tri")
    groups = math.isqrt(tri_count)
    per_group = NB // groups
    half_group = per_group // 2
    strip_rows = stored_tiles.shape[2]
    block_order = stored_tiles.shape[3]
    row_table, col_table = layout(groups, per_group)
    position = lax.axis_index("tri")
    my_cell = jnp.sum(jnp.where(cell_owner == position, jnp.arange(tri_count, dtype=jnp.int32), 0))
    cell_down = my_cell // groups
    cell_across = my_cell % groups
    row_group = jnp.maximum(cell_down, cell_across)
    col_group = jnp.minimum(cell_down, cell_across)
    my_rows = jnp.asarray(row_table)[my_cell]
    my_cols = jnp.asarray(col_table)[my_cell]
    row_local = jnp.clip(my_rows - row_group * per_group, 0, per_group - 1)
    col_local = jnp.clip(my_cols - col_group * per_group, 0, per_group - 1)
    holders = cell_owner[jnp.arange(groups) * groups]
    highest = lax.Precision.HIGHEST
    current = stored_tiles[0]
    lower_slots = np.array([member * half_group for member in range(per_group)], np.int32)
    first_slots = np.array(
        [member * (member + 1) // 2 if member > 0 else 0 for member in range(per_group)], np.int32
    )
    keep_first = np.array([1.0 if member > 0 else 0.0 for member in range(per_group)], np.float32)
    from_lower = current[lower_slots]
    from_first = current[first_slots] * keep_first[:, None, None]
    holder_part = jnp.where(cell_down > 0, from_lower, from_first)
    holder_part = jnp.where(cell_across == 0, holder_part, 0.0).astype(jnp.bfloat16)
    pivot_slot = 0 // 2
    pivot_part = jnp.where(my_cell == 0, current[pivot_slot], 0.0)
    piece_size = holder_part.size // tri_count
    pivot_piece = pivot_part.size // tri_count
    spread_panel = lax.all_to_all(
        holder_part.reshape(tri_count, piece_size), "tri", split_axis=0, concat_axis=0, tiled=True
    )
    spread_pivot = lax.all_to_all(
        pivot_part.reshape(tri_count, pivot_piece).astype(jnp.bfloat16),
        "tri",
        split_axis=0,
        concat_axis=0,
        tiled=True,
    ).astype(jnp.float32)
    picked_panel = spread_panel[holders][:, None, :]
    picked_pivot = spread_pivot[holders[0]][None, :]
    whole_panel = lax.all_gather(picked_panel, "tri", axis=1, tiled=True)
    whole_pivot = lax.all_gather(
        picked_pivot.astype(jnp.bfloat16), "tri", axis=0, tiled=True
    ).astype(picked_pivot.dtype)
    panels = whole_panel.reshape(groups, per_group, strip_rows, block_order)
    pivot_strip = whole_pivot.reshape(strip_rows, block_order)
    own_strips = panels[row_group]
    other_strips = panels[col_group]
    pivot_block = lax.all_gather(
        pivot_strip.astype(jnp.bfloat16), "sub", axis=0, tiled=True
    ).astype(pivot_strip.dtype)
    partner = lax.all_gather(other_strips, "sub", axis=1, tiled=True)
    gram_matrix = jnp.dot(pivot_block.T, pivot_block, precision=highest)
    factor = jnp.linalg.cholesky(gram_matrix)
    column_count = block_order // lax.axis_size("sub")
    first_column = lax.axis_index("sub") * column_count
    columns = lax.dynamic_slice_in_dim(pivot_block.T, first_column, column_count, 1)
    column_part = jax.scipy.linalg.cho_solve((factor, True), columns)
    inverse = lax.all_gather(shortened(column_part), "sub", axis=1, tiled=True).astype(
        column_part.dtype
    )
    scaled = jnp.einsum(
        "irk,kc->irc", own_strips.astype(jnp.float32), inverse, precision=highest
    ).astype(jnp.bfloat16)
    left_slots = scaled[row_local]
    right_slots = partner[col_local]
    update = jnp.einsum("qrk,qck->qrc", left_slots, right_slots, preferred_element_type=jnp.float32)
    live_slots = (my_rows > 0) & (my_cols > 0)
    current = current + jnp.where(live_slots[:, None, None], update, 0.0)
    return current[None]


class Plan:
    def __init__(self, tri, subs, slots, strip, order):
        self.tri, self.subs, self.slots, self.strip, self.order = tri, subs, slots, strip, order
        self.groups = math.isqrt(tri)
        self.per_group = NB // self.groups
        self.half_group = self.per_group // 2
        self.half_tri = tri // 2
        self.piece = strip // self.half_tri
        quarter = self.half_group // 4
        self.wides = [quarter, quarter, 2 * quarter]
        self.firsts = [0, quarter, 2 * quarter]
        self.spreads = [[0, 1], [2]]
        self.o_sub = 0
        self.o_diag = 1
        self.o_me = 2
        self.o_dead = 3
        self.o_src = 8
        self.o_here = self.o_src + self.groups
        self.o_rg = self.o_here + self.groups
        self.o_cg = self.o_rg + self.half_tri
        self.o_hf = self.o_cg + self.half_tri
        self.size = self.o_hf + self.half_tri

    def tiled(self):
        return (
            self.piece % 16 == 0
            and self.order % 128 == 0
            and self.half_group % 4 == 0
            and self.groups * self.groups == self.tri
            and self.half_tri & (self.half_tri - 1) == 0
            and self.subs * self.strip == self.order
            and self.slots == self.per_group * (self.per_group + 1) // 2
        )

    def tiles_of(self, chunk):
        inner = range(self.firsts[chunk], self.firsts[chunk] + self.wides[chunk])
        return [half * self.half_group + n for half in range(2) for n in inner]

    def place_of(self, member):
        for chunk in range(len(self.wides)):
            if member in self.tiles_of(chunk):
                return chunk, self.tiles_of(chunk).index(member)
        raise ValueError(member)

    def column_of(self, inner):
        chunk, place = self.place_of(inner)
        return chunk, 2 * self.wides[chunk] + place


def table_call(p, cell_owner):
    def kernel(owner, out, cell_of):
        position = lax.axis_index("tri")
        for cell in range(p.tri):
            cell_of[owner[cell]] = cell

        def split(cell):
            down = cell // p.groups
            across = cell - down * p.groups
            return down, across

        down, across = split(cell_of[position])
        col_group = jnp.minimum(down, across)
        diag = down == across
        my_half = position // p.half_tri
        out[p.o_sub] = lax.axis_index("sub")
        out[p.o_me] = position - my_half * p.half_tri
        out[p.o_diag] = jnp.where(diag, 1, 0)
        for group in range(p.groups):
            holder = owner[group * p.groups]
            half = holder // p.half_tri
            out[p.o_src + group] = holder - half * p.half_tri
            out[p.o_here + group] = jnp.where(half == my_half, 1, 0)
        for end in range(p.half_tri):
            there_down, there_across = split(cell_of[my_half * p.half_tri + end])
            out[p.o_rg + end] = jnp.maximum(there_down, there_across)
            out[p.o_cg + end] = jnp.minimum(there_down, there_across)
            out[p.o_hf + end] = jnp.where(there_down < there_across, 1, 0)
        out[p.o_dead] = jnp.where((col_group == 0) & (down >= across), 1, 0)

    return pl.pallas_call(
        kernel,
        out_shape=jax.ShapeDtypeStruct((p.size,), jnp.int32),
        in_specs=[pl.BlockSpec(memory_space=pltpu.SMEM)],
        out_specs=pl.BlockSpec(memory_space=pltpu.SMEM),
        scratch_shapes=[pltpu.SMEM((p.tri,), jnp.int32)],
        name="table",
    )(cell_owner)


IN_VMEM = pl.BlockSpec(memory_space=pltpu.VMEM)


def in_vmem(x):
    return pltpu.with_memory_space_constraint(x, pltpu.VMEM)


def limit(mib):
    return pltpu.CompilerParams(vmem_limit_bytes=mib * 2**20)


def in_hbm(x):
    return pltpu.with_memory_space_constraint(x, pltpu.HBM)


def in_hbm(x):
    return pltpu.with_memory_space_constraint(x, pltpu.HBM)


def extract_call(p, cell_owner, current, members, apart):
    one = (len(members), p.piece, p.order)

    def kernel(owner, tiles, *refs):
        outs, (wide, sems) = refs[:-2], refs[-2:]
        position = lax.axis_index("tri")
        me = lax.rem(position, p.half_tri)
        cell = jnp.int32(0)
        for n in range(1, p.tri):
            cell = jnp.where(owner[n] == position, n, cell)
        down = cell // p.groups
        copies = []
        for place, member in enumerate(members):
            slot = jnp.where(down > 0, member * p.half_group, member * (member + 1) // 2)
            copies.append(
                pltpu.make_async_copy(tiles.at[slot], wide.at[place], sems.at[place])
            )
        for copy in copies:
            copy.start()
        for place, copy in enumerate(copies):
            copy.wait()
            if apart:
                for n, out in enumerate(outs):
                    at = pl.multiple_of((me ^ n) * p.piece, p.piece)
                    out[place] = wide[place, pl.ds(at, p.piece)].astype(jnp.bfloat16)
            else:
                rounded = wide[place].astype(jnp.bfloat16)
                outs[0][:, place] = rounded.reshape(p.half_tri, p.piece, p.order)

    if apart:
        out_shape = [pltpu.VMEM(one, jnp.bfloat16)] * p.half_tri
    else:
        out_shape = [pltpu.VMEM((p.half_tri,) + one, jnp.bfloat16)]
    return pl.pallas_call(
        kernel,
        out_shape=out_shape,
        in_specs=[
            pl.BlockSpec(memory_space=pltpu.SMEM),
            pl.BlockSpec(memory_space=pltpu.HBM),
        ],
        out_specs=[IN_VMEM] * len(out_shape),
        scratch_shapes=[
            pltpu.VMEM((len(members), p.strip, p.order), jnp.float32),
            pltpu.SemaphoreType.DMA((len(members),)),
        ],
        compiler_params=limit(8),
        name="extract",
    )(cell_owner, in_hbm(current))


def pick_call(p, table, spread, chunks):
    def kernel(t, *refs):
        sources, outs = refs[: len(spread)], refs[len(spread) :]
        for g in range(p.groups):
            first = 0
            for out in outs:
                count = out.shape[1]
                part = slice(first, first + count)
                first += count
                if len(sources) == 1:
                    out[g] = sources[0][t[p.o_src + g], part]
                    continue
                for n, source in enumerate(sources):

                    @pl.when(t[p.o_src + g] == t[p.o_me] ^ n)
                    def _():
                        out[g] = source[part]

    return pl.pallas_call(
        kernel,
        out_shape=[
            pltpu.VMEM((p.groups, 2 * p.wides[k], p.piece, p.order), jnp.bfloat16) for k in chunks
        ],
        grid_spec=pltpu.PrefetchScalarGridSpec(
            num_scalar_prefetch=1,
            grid=(),
            in_specs=[IN_VMEM] * len(spread),
            out_specs=[IN_VMEM] * len(chunks),
        ),
        compiler_params=limit(8),
        name="pick",
    )(table, *[in_vmem(x) for x in spread])


def build_call(p, table, near, far, wide, with_pivot):
    rows = 3 * wide + (1 if with_pivot else 0)

    def kernel(t, near_ref, far_ref, *outs):
        def part(group, first, count, out, place):
            here = t[p.o_here + group] == 1

            @pl.when(here)
            def _():
                out[place : place + count] = near_ref[group, pl.ds(first, count)]

            @pl.when(jnp.logical_not(here))
            def _():
                out[place : place + count] = far_ref[group, pl.ds(first, count)]

        for n, out in enumerate(outs):
            end = t[p.o_me] ^ n
            part(t[p.o_rg + end], 0, 2 * wide, out, 0)
            part(t[p.o_cg + end], t[p.o_hf + end] * wide, wide, out, 2 * wide)
            if with_pivot:
                part(0, 0, 1, out, 3 * wide)

    return pl.pallas_call(
        kernel,
        out_shape=[pltpu.VMEM((rows, p.piece, p.order), jnp.bfloat16)] * p.half_tri,
        grid_spec=pltpu.PrefetchScalarGridSpec(
            num_scalar_prefetch=1,
            grid=(),
            in_specs=[IN_VMEM, IN_VMEM],
            out_specs=[IN_VMEM] * p.half_tri,
        ),
        compiler_params=limit(8),
        name="build",
    )(table, in_vmem(near), in_vmem(far))


def pack_call(p, table, pieces):
    def kernel(t, *refs):
        out = refs[-1]
        for n in range(p.half_tri):
            out[t[p.o_me] ^ n] = refs[n][...]

    return pl.pallas_call(
        kernel,
        out_shape=pltpu.VMEM((p.half_tri,) + pieces[0].shape, jnp.bfloat16),
        grid_spec=pltpu.PrefetchScalarGridSpec(
            num_scalar_prefetch=1,
            grid=(),
            in_specs=[IN_VMEM] * p.half_tri,
            out_specs=IN_VMEM,
        ),
        compiler_params=limit(8),
        name="pack",
    )(table, *[in_vmem(x) for x in pieces])


def inverse_call(p, table, arrived, current):
    loads = next(n for n in (6, 5, 4, 3, 2, 1) if p.slots % n == 0)
    each = p.slots // loads
    place = 3 * p.wides[0]
    order = p.order

    def kernel(t, *refs):
        sources = refs[: p.subs]
        tiles, high, held, pivot, x_wide, x_half, e_ref, sems = refs[p.subs :]
        copies = [
            pltpu.make_async_copy(
                tiles.at[pl.ds(n * each, each)], held.at[pl.ds(n * each, each)], sems.at[n]
            )
            for n in range(loads)
        ]
        for copy in copies:
            copy.start()
        for shift in range(p.subs):
            strip = lax.rem(t[p.o_sub] + shift, p.subs) * p.strip
            at = pl.multiple_of(strip, p.strip)
            pivot[pl.ds(at, p.strip)] = sources[shift][:, place].reshape(p.strip, order)

        def dot(a, b):
            return lax.dot_general(
                a, b, (((1,), (0,)), ((), ())), preferred_element_type=jnp.float32
            )

        def eye():
            r = lax.broadcasted_iota(jnp.int32, (order, order), 0)
            c = lax.broadcasted_iota(jnp.int32, (order, order), 1)
            return jnp.where(r == c, 1.0, 0.0)

        square = -dot(pivot[...], pivot[...])
        factor = 1.9 / jnp.max(jnp.sum(jnp.abs(square), axis=1))
        residual = eye() - factor * square
        e_ref[...] = residual.astype(jnp.bfloat16)
        wide = -factor * (pivot[...].astype(jnp.float32) + dot(pivot[...], e_ref[...]))
        x_wide[...] = wide
        x_half[...] = wide.astype(jnp.bfloat16)

        def coarse_on(carry):
            step, error, before, noise = carry
            stuck = (before < 1.0) & (error > 0.5 * before)
            return (step < 60) & (error > 3e-3) & (noise < 0.1) & jnp.logical_not(stuck)

        def coarse(carry):
            step, before, _, _ = carry
            x = x_half[...]
            residual = eye() - dot(pivot[...], x)
            e_ref[...] = residual.astype(jnp.bfloat16)
            error = jnp.sum(residual * residual)
            new = x.astype(jnp.float32) + dot(x, e_ref[...])
            x_wide[...] = new
            x_half[...] = new.astype(jnp.bfloat16)
            noise = jnp.sum(new * new) / factor * 2.0**-18
            return step + 1, error, before, noise

        big = jnp.float32(1e30)
        _, reached, _, _ = lax.while_loop(
            coarse_on, coarse, (jnp.int32(0), big, big, jnp.float32(0.0))
        )

        def fine_on(carry):
            step, error, before = carry
            stuck = (before < 0.5) & (error > 0.5 * before)
            return (step < 100) & (error > 1e-4) & jnp.logical_not(stuck)

        def fine(carry):
            step, before, _ = carry
            x = x_wide[...]
            x_high = x.astype(jnp.bfloat16)
            x_low = (x - x_high.astype(jnp.float32)).astype(jnp.bfloat16)
            residual = eye() - (dot(pivot[...], x_high) + dot(pivot[...], x_low))
            error = jnp.sum(residual * residual)
            e_high = residual.astype(jnp.bfloat16)
            e_low = (residual - e_high.astype(jnp.float32)).astype(jnp.bfloat16)
            x_wide[...] = x + (dot(x_high, e_high) + (dot(x_high, e_low) + dot(x_low, e_high)))
            return step + 1, error, before

        @pl.when(jnp.logical_not(reached <= 3e-3))
        def _():
            lax.while_loop(fine_on, fine, (jnp.int32(0), big, big))

        high[...] = x_wide[...].astype(jnp.bfloat16)
        for copy in copies:
            copy.wait()

    square_shape = pltpu.VMEM((order, order), jnp.bfloat16)
    return pl.pallas_call(
        kernel,
        out_shape=(square_shape, pltpu.VMEM(current.shape, jnp.float32)),
        grid_spec=pltpu.PrefetchScalarGridSpec(
            num_scalar_prefetch=1,
            grid=(),
            in_specs=[IN_VMEM] * p.subs + [pl.BlockSpec(memory_space=pltpu.HBM)],
            out_specs=(IN_VMEM, IN_VMEM),
            scratch_shapes=[
                pltpu.VMEM((order, order), jnp.bfloat16),
                pltpu.VMEM((order, order), jnp.float32),
                pltpu.VMEM((order, order), jnp.bfloat16),
                pltpu.VMEM((order, order), jnp.bfloat16),
                pltpu.SemaphoreType.DMA((loads,)),
            ],
        ),
        compiler_params=limit(12),
        cost_estimate=pl.CostEstimate(
            flops=60 * 2 * order**3, bytes_accessed=4 * order**2, transcendentals=0
        ),
        name="inverse",
    )(table, *[in_vmem(x) for x in arrived], in_hbm(current))


def update_call(p, table, held, arrived, inverse, before):
    ring_size = 8
    chunks = len(p.wides)
    early = before is None
    rows_in_box = p.per_group * p.half_group

    def mine(i, j):
        first = max(p.place_of(i)[0], p.place_of(j)[0]) < chunks - 1
        return first == early

    def kernel(t, tiles, inv, *refs):
        at_hand = len(arrived)
        sources = [refs[k * p.subs : (k + 1) * p.subs] for k in range(at_hand)]
        out, column, ring, ring_sems, rest_sem = refs[-5:]
        sub = t[p.o_sub]
        diag = t[p.o_diag] == 1
        dead = t[p.o_dead] == 1

        def strip_of(shift, chunk, place):
            return sources[chunk][shift][:, place].reshape(p.strip, p.order)

        def gather_column(j, chunk, place):
            strips = [strip_of(shift, chunk, place) for shift in range(p.subs)]
            for at in range(p.subs):
                strip = strips[0]
                for shift in range(1, p.subs):
                    here = lax.rem(sub + shift, p.subs) == at
                    strip = jnp.where(here, strips[shift], strip)
                if j == 0:
                    strip = jnp.where(dead, jnp.zeros_like(strip), strip)
                column[j, at * p.strip : (at + 1) * p.strip] = strip

        def scale(members):
            strips = [strip_of(0, *p.place_of(member)) for member in members]
            product = lax.dot_general(
                jnp.concatenate(strips, axis=0),
                inv[...],
                (((1,), (0,)), ((), ())),
                preferred_element_type=jnp.float32,
            )
            return product.astype(jnp.bfloat16)

        def times(left, j):
            return lax.dot_general(
                left, column[j], (((1,), (1,)), ((), ())), preferred_element_type=jnp.float32
            )

        class Writer:
            def __init__(self):
                self.copies = []

            def put(self, slot, product):
                n = len(self.copies)
                if n >= ring_size:
                    self.copies[n - ring_size].wait()
                ring[n % ring_size] = tiles[slot] + product
                copy = pltpu.make_async_copy(
                    ring.at[n % ring_size], out.at[slot], ring_sems.at[n % ring_size]
                )
                copy.start()
                self.copies.append(copy)

            def finish(self):
                for copy in self.copies[-ring_size:]:
                    copy.wait()

        @pl.when(diag)
        def _():
            writer = Writer()
            known = set()

            def column_at(j):
                if j not in known:
                    known.add(j)
                    gather_column(j, *p.place_of(j))

            for i in range(0, p.per_group, 2):
                columns = [j for j in range(i + 2) if mine(i, j)]
                if not columns:
                    continue
                left = scale([i, i + 1])
                for j in columns:
                    column_at(j)
                    if j <= i:
                        product = times(left, j)
                        for r in range(2):
                            slot = (i + r) * (i + r + 1) // 2 + j
                            writer.put(slot, product[r * p.strip : (r + 1) * p.strip])
                    else:
                        slot = (i + 1) * (i + 2) // 2 + j
                        writer.put(slot, times(left[p.strip :], j))
            writer.finish()

        @pl.when(jnp.logical_not(diag))
        def _():
            empty = p.slots - rows_in_box if early else 0
            if empty:
                at = pl.ds(rows_in_box, empty)
                rest = pltpu.make_async_copy(tiles.at[at], out.at[at], rest_sem)
                rest.start()
            writer = Writer()
            known = set()
            for i in range(0, p.per_group, 2):
                columns = [j for j in range(p.half_group) if mine(i, j)]
                if not columns:
                    continue
                left = scale([i, i + 1])
                for j in columns:
                    if j not in known:
                        known.add(j)
                        gather_column(j, *p.column_of(j))
                    product = times(left, j)
                    for r in range(2):
                        slot = (i + r) * p.half_group + j
                        writer.put(slot, product[r * p.strip : (r + 1) * p.strip])
            writer.finish()
            if empty:
                rest.wait()

    hbm = pl.BlockSpec(memory_space=pltpu.HBM)
    delivered = [in_vmem(ref) for chunk in arrived for ref in chunk]
    specs = [IN_VMEM] * (2 + len(delivered))
    return pl.pallas_call(
        kernel,
        out_shape=jax.ShapeDtypeStruct(held.shape, jnp.float32),
        grid_spec=pltpu.PrefetchScalarGridSpec(
            num_scalar_prefetch=1,
            grid=(),
            in_specs=specs if early else specs + [hbm],
            out_specs=hbm,
            scratch_shapes=[
                pltpu.VMEM((p.per_group, p.order, p.order), jnp.bfloat16),
                pltpu.VMEM((ring_size, p.strip, p.order), jnp.float32),
                pltpu.SemaphoreType.DMA((ring_size,)),
                pltpu.SemaphoreType.DMA,
            ],
        ),
        input_output_aliases={} if early else {3 + len(delivered): 0},
        compiler_params=limit(20),
        name="begin" if early else "finish",
    )(
        table,
        in_vmem(held),
        in_vmem(inverse),
        *delivered,
        *([] if early else [before]),
    )


def planned(p, stored_tiles, cell_owner):
    current = stored_tiles[0]
    halves = [list(range(h * p.half_tri, (h + 1) * p.half_tri)) for h in range(2)]
    swap = [(i, (i + p.half_tri) % p.tri) for i in range(p.tri)]
    chunks = len(p.wides)

    def send(pieces):
        arrived = {0: pieces[0]}
        for n in reversed(range(1, p.half_tri)):
            pairs = [(i, i ^ n) for i in range(p.tri)]
            arrived[n] = lax.ppermute(pieces[n], "tri", pairs)
        return [arrived[n] for n in range(p.half_tri)]

    def arrivals(x):
        return [x] + [
            lax.ppermute(x, "sub", [((i + shift) % p.subs, i) for i in range(p.subs)])
            for shift in range(1, p.subs)
        ]

    table = table_call(p, cell_owner)
    near, far, arrived = [], [], []
    for number, members in enumerate(p.spreads):
        tiles = [tile for chunk in members for tile in p.tiles_of(chunk)]
        pieces = extract_call(p, cell_owner, current, tiles, number > 0)
        if number == 0:
            spread = [
                lax.all_to_all(
                    pieces[0],
                    "tri",
                    split_axis=0,
                    concat_axis=0,
                    tiled=True,
                    axis_index_groups=halves,
                )
            ]
        else:
            spread = send(pieces)
        near.extend(pick_call(p, table, spread, members))
    for chunk in range(chunks):
        far.append(lax.ppermute(near[chunk], "tri", swap))
    for chunk in range(chunks):
        built = build_call(p, table, near[chunk], far[chunk], p.wides[chunk], chunk == 0)
        pieces = send(built)
        packed = pack_call(p, table, pieces)
        arrived.append(arrivals(packed))
    inverse, held = inverse_call(p, table, arrived[0], current)
    begun = update_call(p, table, held, arrived[:-1], inverse, None)
    return update_call(p, table, held, arrived, inverse, begun)[None]


def shards(stored_tiles, cell_owner):
    p = Plan(
        lax.axis_size("tri"),
        lax.axis_size("sub"),
        stored_tiles.shape[1],
        stored_tiles.shape[2],
        stored_tiles.shape[3],
    )
    if p.tiled():
        return planned(p, stored_tiles, cell_owner)
    return untiled(stored_tiles, cell_owner)


def solution(mesh):
    placed = (P("tri", None, "sub", None), P())
    return jax.shard_map(
        shards, mesh=mesh, in_specs=placed, out_specs=P("tri", None, "sub", None), check_vma=False
    )
```

profile of v0, /device:TPU:1, one launch (start us, length us, event | category | flops | bytes accessed | tf_op | source)
XLA Modules:
  0.0 151.8 jit_solution(5828597154285873736)
XLA Ops:
  0.0 0.7 copy-done.2
  0.7 3.1 %extract.2 = bf16[8,4,32,512]{3,2,1,0:T(8,128)(2,1)} custom-call(s32[16]{0:T(128)S(1)} %copy-done.2, f32[36,256,512]{2,1,0:T(8,128)} %bitcast.2), custom_call_target="tpu_custom_call" | custom-call | tf_op jit(solution)/shard_map/extract/pallas_call | solution.py:272
  3.8 5.3 %all-to-all-start = ((bf16[8,4,32,512]{3,2,1,0:T(8,128)(2,1)}), bf16[8,4,32,512]{3,2,1,0:T(8,128)(2,1)S(1)}, u32[]{:S(2)}, u32[]{:S(2)}) async-start(bf16[8,4,32,512]{3,2,1,0:T(8,128)(2,1)} %extract.2), calls=%async_computation | async-start | bytes 2097152 | tf_op jit(solution)/shard_map/all_to_all | solution.py:666
  9.1 1.3 table.1.t
  10.4 12.5 %all-to-all-done.refs_0_ = bf16[8,4,32,512]{3,2,1,0:T(8,128)(2,1)S(1)} async-done(((bf16[8,4,32,512]{3,2,1,0:T(8,128)(2,1)}), bf16[8,4,32,512]{3,2,1,0:T(8,128)(2,1)S(1)}, u32[]{:S(2)}, u32[]{:S(2)}) %all-to-all-start) | async-done | bytes 1048608 | tf_op jit(solution)/shard_map/all_to_all | solution.py:666
  23.0 0.7 copy-done
  23.6 0.6 pick.2
  24.2 2.4 %collective-permute-start = (bf16[4,2,32,512]{3,2,1,0:T(8,128)(2,1)S(1)}, bf16[4,2,32,512]{3,2,1,0:T(8,128)(2,1)S(1)}, u32[]{:S(2)}, u32[]{:S(2)}) collective-permute-start(bf16[4,2,32,512]{3,2,1,0:T(8,128)(2,1)S(1)} %get-tuple-element.41.near_ref), channel_id=1, source_target_pairs={{0,16},{2,18},{4,20},{6,22},{8,24},{10,26},{12,28},{14,30},{16,0},... | collective-permute-start | bytes 786440 | tf_op jit(solution)/shard_map/ppermute | solution.py:679
  26.6 2.1 %extract.3 = (bf16[4,32,512]{2,1,0:T(8,128)(2,1)S(1)}, bf16[4,32,512]{2,1,0:T(8,128)(2,1)S(1)}, bf16[4,32,512]{2,1,0:T(8,128)(2,1)S(1)}, bf16[4,32,512]{2,1,0:T(...) custom-call(s32[16]{0:T(128)S(1)} %copy-done.3, ...), custom_call_target="tpu_custom_call" | custom-call | tf_op jit(solution)/shard_map/extract/pallas_call | solution.py:272
  28.8 1.4 collective-permute-start.18
  30.2 0.1 collective-permute-start.19
  30.3 1.2 collective-permute-start.20
  31.5 2.3 %collective-permute-start.21 = (bf16[4,32,512]{2,1,0:T(8,128)(2,1)S(1)}, bf16[4,32,512]{2,1,0:T(8,128)(2,1)S(1)}, u32[]{:S(2)}, u32[]{:S(2)}) collective-permute-start(bf16[4,32,512]{2,1,0:T(8,128)(2,1)S(1)} %get-tuple-element.65), channel_id=1, source_target_pairs={{0,8},{2,10},{4,12},{6,14},{8,0},{10,2},{12,4},{14,6},{16,24},{18,... | collective-permute-start | bytes 393224 | tf_op jit(solution)/shard_map/ppermute | solution.py:650
  33.7 3.3 %collective-permute-done.far_ref = bf16[4,2,32,512]{3,2,1,0:T(8,128)(2,1)S(1)} collective-permute-done((bf16[4,2,32,512]{3,2,1,0:T(8,128)(2,1)S(1)}, bf16[4,2,32,512]{3,2,1,0:T(8,128)(2,1)S(1)}, u32[]{:S(2)}, u32[]{:S(2)}) %collective-permute-start) | collective-permute-done | bytes 262176 | tf_op jit(solution)/shard_map/ppermute | solution.py:679
  37.0 3.5 %collective-permute-start.22 = (bf16[4,32,512]{2,1,0:T(8,128)(2,1)S(1)}, bf16[4,32,512]{2,1,0:T(8,128)(2,1)S(1)}, u32[]{:S(2)}, u32[]{:S(2)}) collective-permute-start(bf16[4,32,512]{2,1,0:T(8,128)(2,1)S(1)} %get-tuple-element.66), channel_id=1, source_target_pairs={{0,10},{2,8},{4,14},{6,12},{8,2},{10,0},{12,6},{14,4},{16,26},{18,... | collective-permute-start | bytes 393224 | tf_op jit(solution)/shard_map/ppermute | solution.py:650
  40.6 1.0 build.3
  41.5 0.0 collective-permute-done.18.refs_1_
  41.6 0.1 collective-permute-start.23
  41.6 2.2 %collective-permute-start.24 = (bf16[4,32,512]{2,1,0:T(8,128)(2,1)S(1)}, bf16[4,32,512]{2,1,0:T(8,128)(2,1)S(1)}, u32[]{:S(2)}, u32[]{:S(2)}) collective-permute-start(bf16[4,32,512]{2,1,0:T(8,128)(2,1)S(1)} %get-tuple-element.68), channel_id=1, source_target_pairs={{0,14},{2,12},{4,10},{6,8},{8,6},{10,4},{12,2},{14,0},{16,30},{18,... | collective-permute-start | bytes 393224 | tf_op jit(solution)/shard_map/ppermute | solution.py:650
  43.8 1.4 collective-permute-start.1
  45.2 0.0 collective-permute-done.21.refs_4_
  45.2 0.1 collective-permute-start.2
  45.3 0.0 collective-permute-done.22.refs_5_
  45.3 1.2 collective-permute-start.3
  46.5 0.3 collective-permute-done.23.refs_6_
  46.8 0.2 collective-permute-start.4
  47.0 2.5 %collective-permute-done.24.refs_7_ = bf16[4,32,512]{2,1,0:T(8,128)(2,1)S(1)} collective-permute-done((bf16[4,32,512]{2,1,0:T(8,128)(2,1)S(1)}, bf16[4,32,512]{2,1,0:T(8,128)(2,1)S(1)}, u32[]{:S(2)}, u32[]{:S(2)}) %collective-permute-start.24) | collective-permute-done | bytes 131104 | tf_op jit(solution)/shard_map/ppermute | solution.py:650
  49.5 1.0 collective-permute-start.5
  50.5 2.5 %collective-permute-start.6 = (bf16[4,32,512]{2,1,0:T(8,128)(2,1)S(1)}, bf16[4,32,512]{2,1,0:T(8,128)(2,1)S(1)}, u32[]{:S(2)}, u32[]{:S(2)}) collective-permute-start(bf16[4,32,512]{2,1,0:T(8,128)(2,1)S(1)} %get-tuple-element.48), channel_id=1, source_target_pairs={{0,12},{2,14},{4,8},{6,10},{8,4},{10,6},{12,0},{14,2},{16,28},{18,... | collective-permute-start | bytes 393224 | tf_op jit(solution)/shard_map/ppermute | solution.py:650
  53.0 3.3 %collective-permute-done.2.refs_2_ = bf16[4,32,512]{2,1,0:T(8,128)(2,1)S(1)} collective-permute-done((bf16[4,32,512]{2,1,0:T(8,128)(2,1)S(1)}, bf16[4,32,512]{2,1,0:T(8,128)(2,1)S(1)}, u32[]{:S(2)}, u32[]{:S(2)}) %collective-permute-start.2) | collective-permute-done | bytes 131104 | tf_op jit(solution)/shard_map/ppermute | solution.py:650
  56.4 0.0 collective-permute-start.7
  56.4 0.8 pick.3.near_ref
  57.2 5.2 %collective-permute-start.25 = (bf16[4,4,32,512]{3,2,1,0:T(8,128)(2,1)S(1)}, bf16[4,4,32,512]{3,2,1,0:T(8,128)(2,1)S(1)}, u32[]{:S(2)}, u32[]{:S(2)}) collective-permute-start(bf16[4,4,32,512]{3,2,1,0:T(8,128)(2,1)S(1)} %pick.3.near_ref), channel_id=1, source_target_pairs={{0,16},{2,18},{4,20},{6,22},{8,24},{10,26},{12,28},{14,30},{16,0},... | collective-permute-start | bytes 1572872 | tf_op jit(solution)/shard_map/ppermute | solution.py:679
  62.5 0.3 collective-permute-done.7.refs_7_
  62.7 0.6 pack.3.refs_0_
  63.3 1.8 %collective-permute-start.8 = (bf16[8,4,32,512]{3,2,1,0:T(8,128)(2,1)S(1)}, bf16[8,4,32,512]{3,2,1,0:T(8,128)(2,1)S(1)}, u32[]{:S(2)}, u32[]{:S(2)}) collective-permute-start(bf16[8,4,32,512]{3,2,1,0:T(8,128)(2,1)S(1)} %pack.3.refs_0_), channel_id=1, source_target_pairs={{1,0},{0,1},{3,2},{2,3},{5,4},{4,5},{7,6},{6,7},{9,8},{8,9},{11,10... | collective-permute-start | bytes 3145736 | tf_op jit(solution)/shard_map/ppermute | solution.py:655
  65.1 4.4 %collective-permute-start.9 = (bf16[4,2,32,512]{3,2,1,0:T(8,128)(2,1)S(1)}, bf16[4,2,32,512]{3,2,1,0:T(8,128)(2,1)S(1)}, u32[]{:S(2)}, u32[]{:S(2)}) collective-permute-start(bf16[4,2,32,512]{3,2,1,0:T(8,128)(2,1)S(1)} %get-tuple-element.52.near_ref), channel_id=1, source_target_pairs={{0,16},{2,18},{4,20},{6,22},{8,24},{10,26},{12,28},{14,30},{16,0},... | collective-permute-start | bytes 786440 | tf_op jit(solution)/shard_map/ppermute | solution.py:679
  69.5 21.1 %collective-permute-done.25.far_ref = bf16[4,4,32,512]{3,2,1,0:T(8,128)(2,1)S(1)} collective-permute-done((bf16[4,4,32,512]{3,2,1,0:T(8,128)(2,1)S(1)}, bf16[4,4,32,512]{3,2,1,0:T(8,128)(2,1)S(1)}, u32[]{:S(2)}, u32[]{:S(2)}) %collective-permute-start.25) | collective-permute-done | bytes 524320 | tf_op jit(solution)/shard_map/ppermute | solution.py:679
  90.6 0.9 build.5
  91.6 2.1 %collective-permute-start.26 = (bf16[6,32,512]{2,1,0:T(8,128)(2,1)S(1)}, bf16[6,32,512]{2,1,0:T(8,128)(2,1)S(1)}, u32[]{:S(2)}, u32[]{:S(2)}) collective-permute-start(bf16[6,32,512]{2,1,0:T(8,128)(2,1)S(1)} %get-tuple-element.70), channel_id=1, source_target_pairs={{0,2},{2,0},{4,6},{6,4},{8,10},{10,8},{12,14},{14,12},{16,18},{18,... | collective-permute-start | bytes 589832 | tf_op jit(solution)/shard_map/ppermute | solution.py:650
  93.6 1.3 collective-permute-start.28
  94.9 2.1 %collective-permute-done.26.refs_1_ = bf16[6,32,512]{2,1,0:T(8,128)(2,1)S(1)} collective-permute-done((bf16[6,32,512]{2,1,0:T(8,128)(2,1)S(1)}, bf16[6,32,512]{2,1,0:T(8,128)(2,1)S(1)}, u32[]{:S(2)}, u32[]{:S(2)}) %collective-permute-start.26) | collective-permute-done | bytes 196640 | tf_op jit(solution)/shard_map/ppermute | solution.py:650
  97.0 3.6 %collective-permute-done.27.refs_2_ = bf16[6,32,512]{2,1,0:T(8,128)(2,1)S(1)} collective-permute-done((bf16[6,32,512]{2,1,0:T(8,128)(2,1)S(1)}, bf16[6,32,512]{2,1,0:T(8,128)(2,1)S(1)}, u32[]{:S(2)}, u32[]{:S(2)}) %collective-permute-start.27) | collective-permute-done | bytes 196640 | tf_op jit(solution)/shard_map/ppermute | solution.py:650
  100.6 0.8 collective-permute-done.28.refs_3_
  101.5 2.4 %collective-permute-start.32 = (bf16[6,32,512]{2,1,0:T(8,128)(2,1)S(1)}, bf16[6,32,512]{2,1,0:T(8,128)(2,1)S(1)}, u32[]{:S(2)}, u32[]{:S(2)}) collective-permute-start(bf16[6,32,512]{2,1,0:T(8,128)(2,1)S(1)} %get-tuple-element.76), channel_id=1, source_target_pairs={{0,14},{2,12},{4,10},{6,8},{8,6},{10,4},{12,2},{14,0},{16,30},{18,... | collective-permute-start | bytes 589832 | tf_op jit(solution)/shard_map/ppermute | solution.py:650
  103.9 0.9 build.4
  104.8 1.2 collective-permute-start.10
  106.0 0.5 collective-permute-done.30.refs_5_
  106.5 1.0 collective-permute-start.11
  107.4 1.6 %collective-permute-done.31.refs_6_ = bf16[6,32,512]{2,1,0:T(8,128)(2,1)S(1)} collective-permute-done((bf16[6,32,512]{2,1,0:T(8,128)(2,1)S(1)}, bf16[6,32,512]{2,1,0:T(8,128)(2,1)S(1)}, u32[]{:S(2)}, u32[]{:S(2)}) %collective-permute-start.31) | collective-permute-done | bytes 196640 | tf_op jit(solution)/shard_map/ppermute | solution.py:650
  109.0 3.2 %collective-permute-start.12 = (bf16[3,32,512]{2,1,0:T(8,128)(2,1)S(1)}, bf16[3,32,512]{2,1,0:T(8,128)(2,1)S(1)}, u32[]{:S(2)}, u32[]{:S(2)}) collective-permute-start(bf16[3,32,512]{2,1,0:T(8,128)(2,1)S(1)} %get-tuple-element.56), channel_id=1, source_target_pairs={{0,6},{2,4},{4,2},{6,0},{8,14},{10,12},{12,10},{14,8},{16,22},{18,... | collective-permute-start | bytes 294920 | tf_op jit(solution)/shard_map/ppermute | solution.py:650
  112.1 1.2 collective-permute-done.32.refs_7_
  113.4 0.9 collective-permute-start.13
  114.3 2.2 %collective-permute-start.14 = (bf16[3,32,512]{2,1,0:T(8,128)(2,1)S(1)}, bf16[3,32,512]{2,1,0:T(8,128)(2,1)S(1)}, u32[]{:S(2)}, u32[]{:S(2)}) collective-permute-start(bf16[3,32,512]{2,1,0:T(8,128)(2,1)S(1)} %get-tuple-element.58), channel_id=1, source_target_pairs={{0,10},{2,8},{4,14},{6,12},{8,2},{10,0},{12,6},{14,4},{16,26},{18,... | collective-permute-start | bytes 294920 | tf_op jit(solution)/shard_map/ppermute | solution.py:650
  116.5 1.6 %collective-permute-start.15 = (bf16[3,32,512]{2,1,0:T(8,128)(2,1)S(1)}, bf16[3,32,512]{2,1,0:T(8,128)(2,1)S(1)}, u32[]{:S(2)}, u32[]{:S(2)}) collective-permute-start(bf16[3,32,512]{2,1,0:T(8,128)(2,1)S(1)} %get-tuple-element.59), channel_id=1, source_target_pairs={{0,12},{2,14},{4,8},{6,10},{8,4},{10,6},{12,0},{14,2},{16,28},{18,... | collective-permute-start | bytes 294920 | tf_op jit(solution)/shard_map/ppermute | solution.py:650
  118.1 0.2 collective-permute-done.12.refs_3_
  118.3 0.7 collective-permute-start.16
  119.0 0.6 pack.5.refs_4_
  119.7 7.4 %collective-permute-start.33 = (bf16[8,6,32,512]{3,2,1,0:T(8,128)(2,1)S(1)}, bf16[8,6,32,512]{3,2,1,0:T(8,128)(2,1)S(1)}, u32[]{:S(2)}, u32[]{:S(2)}) collective-permute-start(bf16[8,6,32,512]{3,2,1,0:T(8,128)(2,1)S(1)} %pack.5.refs_4_), channel_id=1, source_target_pairs={{1,0},{0,1},{3,2},{2,3},{5,4},{4,5},{7,6},{6,7},{9,8},{8,9},{11,10... | collective-permute-start | bytes 4718600 | tf_op jit(solution)/shard_map/ppermute | solution.py:655
  127.1 0.6 pack.4.refs_2_
  127.7 3.8 %collective-permute-start.17 = (bf16[8,3,32,512]{3,2,1,0:T(8,128)(2,1)S(1)}, bf16[8,3,32,512]{3,2,1,0:T(8,128)(2,1)S(1)}, u32[]{:S(2)}, u32[]{:S(2)}) collective-permute-start(bf16[8,3,32,512]{3,2,1,0:T(8,128)(2,1)S(1)} %pack.4.refs_2_), channel_id=1, source_target_pairs={{1,0},{0,1},{3,2},{2,3},{5,4},{4,5},{7,6},{6,7},{9,8},{8,9},{11,10... | collective-permute-start | bytes 2359304 | tf_op jit(solution)/shard_map/ppermute | solution.py:655
  131.5 8.4 %inverse.1 = (bf16[512,512]{1,0:T(8,128)(2,1)S(1)}, f32[36,256,512]{2,1,0:T(8,128)S(1)}) custom-call(s32[40]{0:T(128)S(1)} %copy-done.1, bf16[8,4,32,512]{3,2,1,0:T(8,128)(2,1)S(1)} %pack.3.refs_0_, bf16[8,4,32,512]{3,2,1,0:T(8,128)(2,1)S(1)} %collective-permute-done.8.refs_1_, f32[36,256,512]{2,1,0:T(8,128)} %bitcast.4), custom_call_target="tpu_custom_call" | custom-call | flops 16106127360 | bytes 1048576 | tf_op jit(solution)/shard_map/inverse/pallas_call | solution.py:467
  139.9 3.4 %begin.1.refs_6_ = f32[36,256,512]{2,1,0:T(8,128)} custom-call(s32[40]{0:T(128)S(1)} %copy-done.1, f32[36,256,512]{2,1,0:T(8,128)S(1)} %get-tuple-element.50.tiles, bf16[512,512]{1,0:T(8,128)(2,1)S(1)} %get-tuple-element.51.inv, bf16[8,4,32,512]{3,2,1,0:T(8,128)(2,1)S(1)} %pack.3.refs_0_, bf16[8,4,32,512]{3,2,1,0:T(8,128)(2,1)S(1)} %collective-permute-done.8.refs_1_, ...), custom_call_target="tpu_custom_call" | custom-call | tf_op jit(solution)/shard_map/begin/pallas_call | solution.py:613
  143.3 8.3 %finish.1 = f32[36,256,512]{2,1,0:T(8,128)} custom-call(s32[40]{0:T(128)S(1)} %copy-done.1, f32[36,256,512]{2,1,0:T(8,128)S(1)} %get-tuple-element.50.tiles, bf16[512,512]{1,0:T(8,128)(2,1)S(1)} %get-tuple-element.51.inv, bf16[8,4,32,512]{3,2,1,0:T(8,128)(2,1)S(1)} %pack.3.refs_0_, ...), custom_call_target="tpu_custom_call", output_to_operand_aliasing={{}: (9, {})} | custom-call | tf_op jit(solution)/shard_map/finish/pallas_call | solution.py:613
  (28 shorter events, 0.1 us)
Async XLA Ops:
  0.0 26.6 %copy-start.3 = (s32[16]{0:T(128)S(1)}, s32[16]{0:T(128)}, u32[]{:S(2)}) copy-start(s32[16]{0:T(128)} %owner.5) | copy-start | bytes 196
  0.0 0.7 copy-start.2
  3.8 19.1 %all-to-all-start = ((bf16[8,4,32,512]{3,2,1,0:T(8,128)(2,1)}), bf16[8,4,32,512]{3,2,1,0:T(8,128)(2,1)S(1)}, u32[]{:S(2)}, u32[]{:S(2)}) async-start(bf16[8,4,32,512]{3,2,1,0:T(8,128)(2,1)} %extract.2), calls=%async_computation | async-start | bytes 2097152 | tf_op jit(solution)/shard_map/all_to_all | solution.py:666
  23.0 0.7 copy-start
  23.6 16.9 %copy-start.1 = (s32[40]{0:T(128)S(1)}, s32[40]{0:T(128)}, u32[]{:S(2)}) copy-start(s32[40]{0:T(128)} %table.1.t) | copy-start | bytes 484
  24.2 12.8 %collective-permute-start = (bf16[4,2,32,512]{3,2,1,0:T(8,128)(2,1)S(1)}, bf16[4,2,32,512]{3,2,1,0:T(8,128)(2,1)S(1)}, u32[]{:S(2)}, u32[]{:S(2)}) collective-permute-start(bf16[4,2,32,512]{3,2,1,0:T(8,128)(2,1)S(1)} %get-tuple-element.41.near_ref), channel_id=1, source_target_pairs={{0,16},{2,18},{4,20},{6,22},{8,24},{10,26},{12,28},{14,30},{16,0},... | collective-permute-start | bytes 786440 | tf_op jit(solution)/shard_map/ppermute | solution.py:679
  28.8 12.8 %collective-permute-start.18 = (bf16[4,32,512]{2,1,0:T(8,128)(2,1)S(1)}, bf16[4,32,512]{2,1,0:T(8,128)(2,1)S(1)}, u32[]{:S(2)}, u32[]{:S(2)}) collective-permute-start(bf16[4,32,512]{2,1,0:T(8,128)(2,1)S(1)} %get-tuple-element.62), channel_id=1, source_target_pairs={{0,2},{2,0},{4,6},{6,4},{8,10},{10,8},{12,14},{14,12},{16,18},{18,... | collective-permute-start | bytes 393224 | tf_op jit(solution)/shard_map/ppermute | solution.py:650
  30.2 11.4 %collective-permute-start.19 = (bf16[4,32,512]{2,1,0:T(8,128)(2,1)S(1)}, bf16[4,32,512]{2,1,0:T(8,128)(2,1)S(1)}, u32[]{:S(2)}, u32[]{:S(2)}) collective-permute-start(bf16[4,32,512]{2,1,0:T(8,128)(2,1)S(1)} %get-tuple-element.63), channel_id=1, source_target_pairs={{0,4},{2,6},{4,0},{6,2},{8,12},{10,14},{12,8},{14,10},{16,20},{18,... | collective-permute-start | bytes 393224 | tf_op jit(solution)/shard_map/ppermute | solution.py:650
  30.3 13.5 %collective-permute-start.20 = (bf16[4,32,512]{2,1,0:T(8,128)(2,1)S(1)}, bf16[4,32,512]{2,1,0:T(8,128)(2,1)S(1)}, u32[]{:S(2)}, u32[]{:S(2)}) collective-permute-start(bf16[4,32,512]{2,1,0:T(8,128)(2,1)S(1)} %get-tuple-element.64), channel_id=1, source_target_pairs={{0,6},{2,4},{4,2},{6,0},{8,14},{10,12},{12,10},{14,8},{16,22},{18,... | collective-permute-start | bytes 393224 | tf_op jit(solution)/shard_map/ppermute | solution.py:650
  31.5 13.7 %collective-permute-start.21 = (bf16[4,32,512]{2,1,0:T(8,128)(2,1)S(1)}, bf16[4,32,512]{2,1,0:T(8,128)(2,1)S(1)}, u32[]{:S(2)}, u32[]{:S(2)}) collective-permute-start(bf16[4,32,512]{2,1,0:T(8,128)(2,1)S(1)} %get-tuple-element.65), channel_id=1, source_target_pairs={{0,8},{2,10},{4,12},{6,14},{8,0},{10,2},{12,4},{14,6},{16,24},{18,... | collective-permute-start | bytes 393224 | tf_op jit(solution)/shard_map/ppermute | solution.py:650
  37.0 8.2 %collective-permute-start.22 = (bf16[4,32,512]{2,1,0:T(8,128)(2,1)S(1)}, bf16[4,32,512]{2,1,0:T(8,128)(2,1)S(1)}, u32[]{:S(2)}, u32[]{:S(2)}) collective-permute-start(bf16[4,32,512]{2,1,0:T(8,128)(2,1)S(1)} %get-tuple-element.66), channel_id=1, source_target_pairs={{0,10},{2,8},{4,14},{6,12},{8,2},{10,0},{12,6},{14,4},{16,26},{18,... | collective-permute-start | bytes 393224 | tf_op jit(solution)/shard_map/ppermute | solution.py:650
  41.6 5.3 %collective-permute-start.23 = (bf16[4,32,512]{2,1,0:T(8,128)(2,1)S(1)}, bf16[4,32,512]{2,1,0:T(8,128)(2,1)S(1)}, u32[]{:S(2)}, u32[]{:S(2)}) collective-permute-start(bf16[4,32,512]{2,1,0:T(8,128)(2,1)S(1)} %get-tuple-element.67), channel_id=1, source_target_pairs={{0,12},{2,14},{4,8},{6,10},{8,4},{10,6},{12,0},{14,2},{16,28},{18,... | collective-permute-start | bytes 393224 | tf_op jit(solution)/shard_map/ppermute | solution.py:650
  41.6 7.9 %collective-permute-start.24 = (bf16[4,32,512]{2,1,0:T(8,128)(2,1)S(1)}, bf16[4,32,512]{2,1,0:T(8,128)(2,1)S(1)}, u32[]{:S(2)}, u32[]{:S(2)}) collective-permute-start(bf16[4,32,512]{2,1,0:T(8,128)(2,1)S(1)} %get-tuple-element.68), channel_id=1, source_target_pairs={{0,14},{2,12},{4,10},{6,8},{8,6},{10,4},{12,2},{14,0},{16,30},{18,... | collective-permute-start | bytes 393224 | tf_op jit(solution)/shard_map/ppermute | solution.py:650
  43.8 6.7 %collective-permute-start.1 = (bf16[4,32,512]{2,1,0:T(8,128)(2,1)S(1)}, bf16[4,32,512]{2,1,0:T(8,128)(2,1)S(1)}, u32[]{:S(2)}, u32[]{:S(2)}) collective-permute-start(bf16[4,32,512]{2,1,0:T(8,128)(2,1)S(1)} %get-tuple-element.43), channel_id=1, source_target_pairs={{0,2},{2,0},{4,6},{6,4},{8,10},{10,8},{12,14},{14,12},{16,18},{18,... | collective-permute-start | bytes 393224 | tf_op jit(solution)/shard_map/ppermute | solution.py:650
  45.2 11.2 %collective-permute-start.2 = (bf16[4,32,512]{2,1,0:T(8,128)(2,1)S(1)}, bf16[4,32,512]{2,1,0:T(8,128)(2,1)S(1)}, u32[]{:S(2)}, u32[]{:S(2)}) collective-permute-start(bf16[4,32,512]{2,1,0:T(8,128)(2,1)S(1)} %get-tuple-element.44), channel_id=1, source_target_pairs={{0,4},{2,6},{4,0},{6,2},{8,12},{10,14},{12,8},{14,10},{16,20},{18,... | collective-permute-start | bytes 393224 | tf_op jit(solution)/shard_map/ppermute | solution.py:650
  45.3 11.9 %collective-permute-start.3 = (bf16[4,32,512]{2,1,0:T(8,128)(2,1)S(1)}, bf16[4,32,512]{2,1,0:T(8,128)(2,1)S(1)}, u32[]{:S(2)}, u32[]{:S(2)}) collective-permute-start(bf16[4,32,512]{2,1,0:T(8,128)(2,1)S(1)} %get-tuple-element.45), channel_id=1, source_target_pairs={{0,6},{2,4},{4,2},{6,0},{8,14},{10,12},{12,10},{14,8},{16,22},{18,... | collective-permute-start | bytes 393224 | tf_op jit(solution)/shard_map/ppermute | solution.py:650
  46.8 15.6 %collective-permute-start.4 = (bf16[4,32,512]{2,1,0:T(8,128)(2,1)S(1)}, bf16[4,32,512]{2,1,0:T(8,128)(2,1)S(1)}, u32[]{:S(2)}, u32[]{:S(2)}) collective-permute-start(bf16[4,32,512]{2,1,0:T(8,128)(2,1)S(1)} %get-tuple-element.46), channel_id=1, source_target_pairs={{0,8},{2,10},{4,12},{6,14},{8,0},{10,2},{12,4},{14,6},{16,24},{18,... | collective-permute-start | bytes 393224 | tf_op jit(solution)/shard_map/ppermute | solution.py:650
  49.5 12.9 %collective-permute-start.5 = (bf16[4,32,512]{2,1,0:T(8,128)(2,1)S(1)}, bf16[4,32,512]{2,1,0:T(8,128)(2,1)S(1)}, u32[]{:S(2)}, u32[]{:S(2)}) collective-permute-start(bf16[4,32,512]{2,1,0:T(8,128)(2,1)S(1)} %get-tuple-element.47), channel_id=1, source_target_pairs={{0,10},{2,8},{4,14},{6,12},{8,2},{10,0},{12,6},{14,4},{16,26},{18,... | collective-permute-start | bytes 393224 | tf_op jit(solution)/shard_map/ppermute | solution.py:650
  50.5 11.9 %collective-permute-start.6 = (bf16[4,32,512]{2,1,0:T(8,128)(2,1)S(1)}, bf16[4,32,512]{2,1,0:T(8,128)(2,1)S(1)}, u32[]{:S(2)}, u32[]{:S(2)}) collective-permute-start(bf16[4,32,512]{2,1,0:T(8,128)(2,1)S(1)} %get-tuple-element.48), channel_id=1, source_target_pairs={{0,12},{2,14},{4,8},{6,10},{8,4},{10,6},{12,0},{14,2},{16,28},{18,... | collective-permute-start | bytes 393224 | tf_op jit(solution)/shard_map/ppermute | solution.py:650
  56.4 6.4 %collective-permute-start.7 = (bf16[4,32,512]{2,1,0:T(8,128)(2,1)S(1)}, bf16[4,32,512]{2,1,0:T(8,128)(2,1)S(1)}, u32[]{:S(2)}, u32[]{:S(2)}) collective-permute-start(bf16[4,32,512]{2,1,0:T(8,128)(2,1)S(1)} %get-tuple-element.49), channel_id=1, source_target_pairs={{0,14},{2,12},{4,10},{6,8},{8,6},{10,4},{12,2},{14,0},{16,30},{18,... | collective-permute-start | bytes 393224 | tf_op jit(solution)/shard_map/ppermute | solution.py:650
  57.2 33.4 %collective-permute-start.25 = (bf16[4,4,32,512]{3,2,1,0:T(8,128)(2,1)S(1)}, bf16[4,4,32,512]{3,2,1,0:T(8,128)(2,1)S(1)}, u32[]{:S(2)}, u32[]{:S(2)}) collective-permute-start(bf16[4,4,32,512]{3,2,1,0:T(8,128)(2,1)S(1)} %pick.3.near_ref), channel_id=1, source_target_pairs={{0,16},{2,18},{4,20},{6,22},{8,24},{10,26},{12,28},{14,30},{16,0},... | collective-permute-start | bytes 1572872 | tf_op jit(solution)/shard_map/ppermute | solution.py:679
  63.3 68.2 %collective-permute-start.8 = (bf16[8,4,32,512]{3,2,1,0:T(8,128)(2,1)S(1)}, bf16[8,4,32,512]{3,2,1,0:T(8,128)(2,1)S(1)}, u32[]{:S(2)}, u32[]{:S(2)}) collective-permute-start(bf16[8,4,32,512]{3,2,1,0:T(8,128)(2,1)S(1)} %pack.3.refs_0_), channel_id=1, source_target_pairs={{1,0},{0,1},{3,2},{2,3},{5,4},{4,5},{7,6},{6,7},{9,8},{8,9},{11,10... | collective-permute-start | bytes 3145736 | tf_op jit(solution)/shard_map/ppermute | solution.py:655
  65.1 36.3 %collective-permute-start.9 = (bf16[4,2,32,512]{3,2,1,0:T(8,128)(2,1)S(1)}, bf16[4,2,32,512]{3,2,1,0:T(8,128)(2,1)S(1)}, u32[]{:S(2)}, u32[]{:S(2)}) collective-permute-start(bf16[4,2,32,512]{3,2,1,0:T(8,128)(2,1)S(1)} %get-tuple-element.52.near_ref), channel_id=1, source_target_pairs={{0,16},{2,18},{4,20},{6,22},{8,24},{10,26},{12,28},{14,30},{16,0},... | collective-permute-start | bytes 786440 | tf_op jit(solution)/shard_map/ppermute | solution.py:679
  91.6 5.4 %collective-permute-start.26 = (bf16[6,32,512]{2,1,0:T(8,128)(2,1)S(1)}, bf16[6,32,512]{2,1,0:T(8,128)(2,1)S(1)}, u32[]{:S(2)}, u32[]{:S(2)}) collective-permute-start(bf16[6,32,512]{2,1,0:T(8,128)(2,1)S(1)} %get-tuple-element.70), channel_id=1, source_target_pairs={{0,2},{2,0},{4,6},{6,4},{8,10},{10,8},{12,14},{14,12},{16,18},{18,... | collective-permute-start | bytes 589832 | tf_op jit(solution)/shard_map/ppermute | solution.py:650
  93.6 7.0 %collective-permute-start.27 = (bf16[6,32,512]{2,1,0:T(8,128)(2,1)S(1)}, bf16[6,32,512]{2,1,0:T(8,128)(2,1)S(1)}, u32[]{:S(2)}, u32[]{:S(2)}) collective-permute-start(bf16[6,32,512]{2,1,0:T(8,128)(2,1)S(1)} %get-tuple-element.71), channel_id=1, source_target_pairs={{0,4},{2,6},{4,0},{6,2},{8,12},{10,14},{12,8},{14,10},{16,20},{18,... | collective-permute-start | bytes 589832 | tf_op jit(solution)/shard_map/ppermute | solution.py:650
  93.6 7.8 %collective-permute-start.28 = (bf16[6,32,512]{2,1,0:T(8,128)(2,1)S(1)}, bf16[6,32,512]{2,1,0:T(8,128)(2,1)S(1)}, u32[]{:S(2)}, u32[]{:S(2)}) collective-permute-start(bf16[6,32,512]{2,1,0:T(8,128)(2,1)S(1)} %get-tuple-element.72), channel_id=1, source_target_pairs={{0,6},{2,4},{4,2},{6,0},{8,14},{10,12},{12,10},{14,8},{16,22},{18,... | collective-permute-start | bytes 589832 | tf_op jit(solution)/shard_map/ppermute | solution.py:650
  97.0 7.8 %collective-permute-start.29 = (bf16[6,32,512]{2,1,0:T(8,128)(2,1)S(1)}, bf16[6,32,512]{2,1,0:T(8,128)(2,1)S(1)}, u32[]{:S(2)}, u32[]{:S(2)}) collective-permute-start(bf16[6,32,512]{2,1,0:T(8,128)(2,1)S(1)} %get-tuple-element.73), channel_id=1, source_target_pairs={{0,8},{2,10},{4,12},{6,14},{8,0},{10,2},{12,4},{14,6},{16,24},{18,... | collective-permute-start | bytes 589832 | tf_op jit(solution)/shard_map/ppermute | solution.py:650
  100.6 5.9 %collective-permute-start.30 = (bf16[6,32,512]{2,1,0:T(8,128)(2,1)S(1)}, bf16[6,32,512]{2,1,0:T(8,128)(2,1)S(1)}, u32[]{:S(2)}, u32[]{:S(2)}) collective-permute-start(bf16[6,32,512]{2,1,0:T(8,128)(2,1)S(1)} %get-tuple-element.74), channel_id=1, source_target_pairs={{0,10},{2,8},{4,14},{6,12},{8,2},{10,0},{12,6},{14,4},{16,26},{18,... | collective-permute-start | bytes 589832 | tf_op jit(solution)/shard_map/ppermute | solution.py:650
  101.4 7.5 %collective-permute-start.31 = (bf16[6,32,512]{2,1,0:T(8,128)(2,1)S(1)}, bf16[6,32,512]{2,1,0:T(8,128)(2,1)S(1)}, u32[]{:S(2)}, u32[]{:S(2)}) collective-permute-start(bf16[6,32,512]{2,1,0:T(8,128)(2,1)S(1)} %get-tuple-element.75), channel_id=1, source_target_pairs={{0,12},{2,14},{4,8},{6,10},{8,4},{10,6},{12,0},{14,2},{16,28},{18,... | collective-permute-start | bytes 589832 | tf_op jit(solution)/shard_map/ppermute | solution.py:650
  101.5 11.9 %collective-permute-start.32 = (bf16[6,32,512]{2,1,0:T(8,128)(2,1)S(1)}, bf16[6,32,512]{2,1,0:T(8,128)(2,1)S(1)}, u32[]{:S(2)}, u32[]{:S(2)}) collective-permute-start(bf16[6,32,512]{2,1,0:T(8,128)(2,1)S(1)} %get-tuple-element.76), channel_id=1, source_target_pairs={{0,14},{2,12},{4,10},{6,8},{8,6},{10,4},{12,2},{14,0},{16,30},{18,... | collective-permute-start | bytes 589832 | tf_op jit(solution)/shard_map/ppermute | solution.py:650
  104.8 9.5 %collective-permute-start.10 = (bf16[3,32,512]{2,1,0:T(8,128)(2,1)S(1)}, bf16[3,32,512]{2,1,0:T(8,128)(2,1)S(1)}, u32[]{:S(2)}, u32[]{:S(2)}) collective-permute-start(bf16[3,32,512]{2,1,0:T(8,128)(2,1)S(1)} %get-tuple-element.54), channel_id=1, source_target_pairs={{0,2},{2,0},{4,6},{6,4},{8,10},{10,8},{12,14},{14,12},{16,18},{18,... | collective-permute-start | bytes 294920 | tf_op jit(solution)/shard_map/ppermute | solution.py:650
  106.5 10.0 %collective-permute-start.11 = (bf16[3,32,512]{2,1,0:T(8,128)(2,1)S(1)}, bf16[3,32,512]{2,1,0:T(8,128)(2,1)S(1)}, u32[]{:S(2)}, u32[]{:S(2)}) collective-permute-start(bf16[3,32,512]{2,1,0:T(8,128)(2,1)S(1)} %get-tuple-element.55), channel_id=1, source_target_pairs={{0,4},{2,6},{4,0},{6,2},{8,12},{10,14},{12,8},{14,10},{16,20},{18,... | collective-permute-start | bytes 294920 | tf_op jit(solution)/shard_map/ppermute | solution.py:650
  109.0 9.3 %collective-permute-start.12 = (bf16[3,32,512]{2,1,0:T(8,128)(2,1)S(1)}, bf16[3,32,512]{2,1,0:T(8,128)(2,1)S(1)}, u32[]{:S(2)}, u32[]{:S(2)}) collective-permute-start(bf16[3,32,512]{2,1,0:T(8,128)(2,1)S(1)} %get-tuple-element.56), channel_id=1, source_target_pairs={{0,6},{2,4},{4,2},{6,0},{8,14},{10,12},{12,10},{14,8},{16,22},{18,... | collective-permute-start | bytes 294920 | tf_op jit(solution)/shard_map/ppermute | solution.py:650
  113.4 6.3 %collective-permute-start.13 = (bf16[3,32,512]{2,1,0:T(8,128)(2,1)S(1)}, bf16[3,32,512]{2,1,0:T(8,128)(2,1)S(1)}, u32[]{:S(2)}, u32[]{:S(2)}) collective-permute-start(bf16[3,32,512]{2,1,0:T(8,128)(2,1)S(1)} %get-tuple-element.57), channel_id=1, source_target_pairs={{0,8},{2,10},{4,12},{6,14},{8,0},{10,2},{12,4},{14,6},{16,24},{18,... | collective-permute-start | bytes 294920 | tf_op jit(solution)/shard_map/ppermute | solution.py:650
  114.3 12.8 %collective-permute-start.14 = (bf16[3,32,512]{2,1,0:T(8,128)(2,1)S(1)}, bf16[3,32,512]{2,1,0:T(8,128)(2,1)S(1)}, u32[]{:S(2)}, u32[]{:S(2)}) collective-permute-start(bf16[3,32,512]{2,1,0:T(8,128)(2,1)S(1)} %get-tuple-element.58), channel_id=1, source_target_pairs={{0,10},{2,8},{4,14},{6,12},{8,2},{10,0},{12,6},{14,4},{16,26},{18,... | collective-permute-start | bytes 294920 | tf_op jit(solution)/shard_map/ppermute | solution.py:650
  116.5 10.6 %collective-permute-start.15 = (bf16[3,32,512]{2,1,0:T(8,128)(2,1)S(1)}, bf16[3,32,512]{2,1,0:T(8,128)(2,1)S(1)}, u32[]{:S(2)}, u32[]{:S(2)}) collective-permute-start(bf16[3,32,512]{2,1,0:T(8,128)(2,1)S(1)} %get-tuple-element.59), channel_id=1, source_target_pairs={{0,12},{2,14},{4,8},{6,10},{8,4},{10,6},{12,0},{14,2},{16,28},{18,... | collective-permute-start | bytes 294920 | tf_op jit(solution)/shard_map/ppermute | solution.py:650
  118.3 8.8 %collective-permute-start.16 = (bf16[3,32,512]{2,1,0:T(8,128)(2,1)S(1)}, bf16[3,32,512]{2,1,0:T(8,128)(2,1)S(1)}, u32[]{:S(2)}, u32[]{:S(2)}) collective-permute-start(bf16[3,32,512]{2,1,0:T(8,128)(2,1)S(1)} %get-tuple-element.60), channel_id=1, source_target_pairs={{0,14},{2,12},{4,10},{6,8},{8,6},{10,4},{12,2},{14,0},{16,30},{18,... | collective-permute-start | bytes 294920 | tf_op jit(solution)/shard_map/ppermute | solution.py:650
  119.7 23.6 %collective-permute-start.33 = (bf16[8,6,32,512]{3,2,1,0:T(8,128)(2,1)S(1)}, bf16[8,6,32,512]{3,2,1,0:T(8,128)(2,1)S(1)}, u32[]{:S(2)}, u32[]{:S(2)}) collective-permute-start(bf16[8,6,32,512]{3,2,1,0:T(8,128)(2,1)S(1)} %pack.5.refs_4_), channel_id=1, source_target_pairs={{1,0},{0,1},{3,2},{2,3},{5,4},{4,5},{7,6},{6,7},{9,8},{8,9},{11,10... | collective-permute-start | bytes 4718600 | tf_op jit(solution)/shard_map/ppermute | solution.py:655
  127.7 12.1 %collective-permute-start.17 = (bf16[8,3,32,512]{3,2,1,0:T(8,128)(2,1)S(1)}, bf16[8,3,32,512]{3,2,1,0:T(8,128)(2,1)S(1)}, u32[]{:S(2)}, u32[]{:S(2)}) collective-permute-start(bf16[8,3,32,512]{3,2,1,0:T(8,128)(2,1)S(1)} %pack.4.refs_2_), channel_id=1, source_target_pairs={{1,0},{0,1},{3,2},{2,3},{5,4},{4,5},{7,6},{6,7},{9,8},{8,9},{11,10... | collective-permute-start | bytes 2359304 | tf_op jit(solution)/shard_map/ppermute | solution.py:655
where the time goes:
time: 152 us
  starting transfers between devices  63.9 us (42%)
  waiting for transfers between devices  53.5 us (35%)
  Pallas kernels  32.6 us (21%)
    ppermute x28, starting transfers between devices, send(): arrived[n] = lax.ppermute(pieces[n], 'tri', pairs)  33.6 us
    ppermute x3, waiting for transfers between devices, planned(): far.append(lax.ppermute(near[chunk], 'tri', swap))  24.4 us
    ppermute x28, waiting for transfers between devices, send(): arrived[n] = lax.ppermute(pieces[n], 'tri', pairs)  16.6 us
    ppermute x3, starting transfers between devices, arrivals(): lax.ppermute(x, 'sub', [((i + shift) % p.subs, i) for i in range(p.subs)])  13 us
    all_to_all x1, waiting for transfers between devices, planned(): lax.all_to_all(pieces[0], 'tri', split_axis=0, concat_axis=0, tiled=True,...  12.5 us
    ppermute x3, starting transfers between devices, planned(): far.append(lax.ppermute(near[chunk], 'tri', swap))  12.1 us
    pallas_call x2, Pallas kernels, update_call(): pl.pallas_call(kernel, out_shape=jax.ShapeDtypeStruct(held.shape, jnp.flo...  11.7 us
    pallas_call x1, Pallas kernels, inverse_call(): pl.pallas_call(kernel, out_shape=(square_shape, pltpu.VMEM(current.shape,...  8.36 us
  transfers between devices with their start and end apart: 35, of which 14 were waited for; matrix products, arithmetic and copies ran while one was open for 0% of the time, Pallas kernels for 14%

commit v1 on v0

--- a/solution.py
+++ b/solution.py
@@ -136,10 +136,9 @@
         self.half_group = self.per_group // 2
         self.half_tri = tri // 2
         self.piece = strip // self.half_tri
-        quarter = self.half_group // 4
-        self.wides = [quarter, quarter, 2 * quarter]
-        self.firsts = [0, quarter, 2 * quarter]
-        self.spreads = [[0, 1], [2]]
+        self.quarter = self.half_group // 4
+        self.spreads = [[0, 1], [2, 3]]
+        self.deliveries = [[0], [1, 2], [3]]
         self.o_sub = 0
         self.o_diag = 1
         self.o_me = 2
@@ -162,19 +161,25 @@
             and self.slots == self.per_group * (self.per_group + 1) // 2
         )
 
-    def tiles_of(self, chunk):
-        inner = range(self.firsts[chunk], self.firsts[chunk] + self.wides[chunk])
+    def tiles_of(self, unit):
+        inner = range(unit * self.quarter, (unit + 1) * self.quarter)
         return [half * self.half_group + n for half in range(2) for n in inner]
 
+    def unit_of(self, inner):
+        unit, rest = divmod(inner, self.quarter)
+        for chunk, units in enumerate(self.deliveries):
+            if unit in units:
+                return chunk, 3 * self.quarter * units.index(unit), rest
+        raise ValueError(inner)
+
     def place_of(self, member):
-        for chunk in range(len(self.wides)):
-            if member in self.tiles_of(chunk):
-                return chunk, self.tiles_of(chunk).index(member)
-        raise ValueError(member)
+        half, inner = divmod(member, self.half_group)
+        chunk, first, rest = self.unit_of(inner)
+        return chunk, first + half * self.quarter + rest
 
     def column_of(self, inner):
-        chunk, place = self.place_of(inner)
-        return chunk, 2 * self.wides[chunk] + place
+        chunk, first, rest = self.unit_of(inner)
+        return chunk, first + 2 * self.quarter + rest
 
 
 def table_call(p, cell_owner):
@@ -286,7 +291,7 @@
     )(cell_owner, in_hbm(current))
 
 
-def pick_call(p, table, spread, chunks):
+def pick_call(p, table, spread, units):
     def kernel(t, *refs):
         sources, outs = refs[: len(spread)], refs[len(spread) :]
         for g in range(p.groups):
@@ -307,40 +312,46 @@
     return pl.pallas_call(
         kernel,
         out_shape=[
-            pltpu.VMEM((p.groups, 2 * p.wides[k], p.piece, p.order), jnp.bfloat16) for k in chunks
+            pltpu.VMEM((p.groups, 2 * p.quarter, p.piece, p.order), jnp.bfloat16) for _ in units
         ],
         grid_spec=pltpu.PrefetchScalarGridSpec(
             num_scalar_prefetch=1,
             grid=(),
             in_specs=[IN_VMEM] * len(spread),
-            out_specs=[IN_VMEM] * len(chunks),
+            out_specs=[IN_VMEM] * len(units),
         ),
         compiler_params=limit(8),
         name="pick",
     )(table, *[in_vmem(x) for x in spread])
 
 
-def build_call(p, table, near, far, wide, with_pivot):
-    rows = 3 * wide + (1 if with_pivot else 0)
-
-    def kernel(t, near_ref, far_ref, *outs):
-        def part(group, first, count, out, place):
+def build_call(p, table, near, far, with_pivot):
+    wide = p.quarter
+    rows = 3 * wide * len(near) + (1 if with_pivot else 0)
+
+    def kernel(t, *refs):
+        near_refs, far_refs = refs[: len(near)], refs[len(near) : 2 * len(near)]
+        outs = refs[2 * len(near) :]
+
+        def part(unit, group, first, count, out, place):
             here = t[p.o_here + group] == 1
 
             @pl.when(here)
             def _():
-                out[place : place + count] = near_ref[group, pl.ds(first, count)]
+                out[place : place + count] = near_refs[unit][group, pl.ds(first, count)]
 
             @pl.when(jnp.logical_not(here))
             def _():
-                out[place : place + count] = far_ref[group, pl.ds(first, count)]
+                out[place : place + count] = far_refs[unit][group, pl.ds(first, count)]
 
         for n, out in enumerate(outs):
             end = t[p.o_me] ^ n
-            part(t[p.o_rg + end], 0, 2 * wide, out, 0)
-            part(t[p.o_cg + end], t[p.o_hf + end] * wide, wide, out, 2 * wide)
+            for unit in range(len(near)):
+                at = 3 * wide * unit
+                part(unit, t[p.o_rg + end], 0, 2 * wide, out, at)
+                part(unit, t[p.o_cg + end], t[p.o_hf + end] * wide, wide, out, at + 2 * wide)
             if with_pivot:
-                part(0, 0, 1, out, 3 * wide)
+                part(0, 0, 0, 1, out, rows - 1)
 
     return pl.pallas_call(
         kernel,
@@ -348,12 +359,12 @@
         grid_spec=pltpu.PrefetchScalarGridSpec(
             num_scalar_prefetch=1,
             grid=(),
-            in_specs=[IN_VMEM, IN_VMEM],
+            in_specs=[IN_VMEM] * (2 * len(near)),
             out_specs=[IN_VMEM] * p.half_tri,
         ),
         compiler_params=limit(8),
         name="build",
-    )(table, in_vmem(near), in_vmem(far))
+    )(table, *[in_vmem(x) for x in near], *[in_vmem(x) for x in far])
 
 
 def pack_call(p, table, pieces):
@@ -379,7 +390,7 @@
 def inverse_call(p, table, arrived, current):
     loads = next(n for n in (6, 5, 4, 3, 2, 1) if p.slots % n == 0)
     each = p.slots // loads
-    place = 3 * p.wides[0]
+    place = 3 * p.quarter * len(p.deliveries[0])
     order = p.order
 
     def kernel(t, *refs):
@@ -490,9 +501,14 @@
 
 def update_call(p, table, held, arrived, inverse, before):
     ring_size = 8
-    chunks = len(p.wides)
+    chunks = len(p.deliveries)
     early = before is None
     rows_in_box = p.per_group * p.half_group
+
+    members = range(p.per_group)
+    known_first = [i for i in members if p.place_of(i)[0] < chunks - 1]
+    known_last = [i for i in members if i not in known_first]
+    row_sets = [some[n : n + 2] for some in (known_first, known_last) for n in range(0, len(some), 2)]
 
     def mine(i, j):
         first = max(p.place_of(i)[0], p.place_of(j)[0]) < chunks - 1
@@ -564,21 +580,18 @@
                     known.add(j)
                     gather_column(j, *p.place_of(j))
 
-            for i in range(0, p.per_group, 2):
-                columns = [j for j in range(i + 2) if mine(i, j)]
+            for rows in row_sets:
+                columns = [j for j in range(rows[-1] + 1) if mine(rows[0], j)]
                 if not columns:
                     continue
-                left = scale([i, i + 1])
+                left = scale(rows)
                 for j in columns:
                     column_at(j)
-                    if j <= i:
-                        product = times(left, j)
-                        for r in range(2):
-                            slot = (i + r) * (i + r + 1) // 2 + j
-                            writer.put(slot, product[r * p.strip : (r + 1) * p.strip])
-                    else:
-                        slot = (i + 1) * (i + 2) // 2 + j
-                        writer.put(slot, times(left[p.strip :], j))
+                    live = [row for row in rows if j <= row]
+                    product = times(left[(len(rows) - len(live)) * p.strip :], j)
+                    for r, row in enumerate(live):
+                        slot = row * (row + 1) // 2 + j
+                        writer.put(slot, product[r * p.strip : (r + 1) * p.strip])
             writer.finish()
 
         @pl.when(jnp.logical_not(diag))
@@ -590,18 +603,18 @@
                 rest.start()
             writer = Writer()
             known = set()
-            for i in range(0, p.per_group, 2):
-                columns = [j for j in range(p.half_group) if mine(i, j)]
+            for rows in row_sets:
+                columns = [j for j in range(p.half_group) if mine(rows[0], j)]
                 if not columns:
                     continue
-                left = scale([i, i + 1])
+                left = scale(rows)
                 for j in columns:
                     if j not in known:
                         known.add(j)
                         gather_column(j, *p.column_of(j))
                     product = times(left, j)
-                    for r in range(2):
-                        slot = (i + r) * p.half_group + j
+                    for r, row in enumerate(rows):
+                        slot = row * p.half_group + j
                         writer.put(slot, product[r * p.strip : (r + 1) * p.strip])
             writer.finish()
             if empty:
@@ -641,7 +654,6 @@
     current = stored_tiles[0]
     halves = [list(range(h * p.half_tri, (h + 1) * p.half_tri)) for h in range(2)]
     swap = [(i, (i + p.half_tri) % p.tri) for i in range(p.tri)]
-    chunks = len(p.wides)
 
     def send(pieces):
         arrived = {0: pieces[0]}
@@ -659,7 +671,7 @@
     table = table_call(p, cell_owner)
     near, far, arrived = [], [], []
     for number, members in enumerate(p.spreads):
-        tiles = [tile for chunk in members for tile in p.tiles_of(chunk)]
+        tiles = [tile for unit in members for tile in p.tiles_of(unit)]
         pieces = extract_call(p, cell_owner, current, tiles, number > 0)
         if number == 0:
             spread = [
@@ -675,10 +687,10 @@
         else:
             spread = send(pieces)
         near.extend(pick_call(p, table, spread, members))
-    for chunk in range(chunks):
-        far.append(lax.ppermute(near[chunk], "tri", swap))
-    for chunk in range(chunks):
-        built = build_call(p, table, near[chunk], far[chunk], p.wides[chunk], chunk == 0)
+    for x in near:
+        far.append(lax.ppermute(x, "tri", swap))
+    for chunk, units in enumerate(p.deliveries):
+        built = build_call(p, table, [near[u] for u in units], [far[u] for u in units], chunk == 0)
         pieces = send(built)
         packed = pack_call(p, table, pieces)
         arrived.append(arrivals(packed))

time: 152 us -> 176 us (1.16)
  waiting for transfers between devices: 53.5 us -> 84.6 us
  starting transfers between devices: 63.9 us -> 55.8 us
    ppermute x3 -> x4, waiting for transfers between devices: 24.4 us -> 41.6 us  [planned(): far.append(lax.ppermute(x, 'tri', swap))]
    ppermute x28, waiting for transfers between devices: 16.6 us -> 30.5 us  [send(): arrived[n] = lax.ppermute(pieces[n], 'tri', pairs)]
    ppermute x3 -> x4, starting transfers between devices: 12.1 us -> 7.37 us  [planned(): far.append(lax.ppermute(x, 'tri', swap))]
    ppermute x28, starting transfers between devices: 33.6 us -> 31.1 us  [send(): arrived[n] = lax.ppermute(pieces[n], 'tri', pairs)]
  transfers between devices with their start and end apart: 35 -> 36, of which waited for: 14 -> 15; matrix products, arithmetic and copies ran while one was open for 0% -> 0% of each run, Pallas kernels for 14% -> 13%
where the time goes in v1:
time: 176 us
  waiting for transfers between devices  84.6 us (48%)
  starting transfers between devices  55.8 us (32%)
  Pallas kernels  33.6 us (19%)
    ppermute x4, waiting for transfers between devices, planned(): far.append(lax.ppermute(x, 'tri', swap))  41.6 us
    ppermute x28, starting transfers between devices, send(): arrived[n] = lax.ppermute(pieces[n], 'tri', pairs)  31.1 us
    ppermute x28, waiting for transfers between devices, send(): arrived[n] = lax.ppermute(pieces[n], 'tri', pairs)  30.5 us
    all_to_all x1, waiting for transfers between devices, planned(): lax.all_to_all(pieces[0], 'tri', split_axis=0, concat_axis=0, tiled=True,...  12.5 us
    pallas_call x2, Pallas kernels, update_call(): pl.pallas_call(kernel, out_shape=jax.ShapeDtypeStruct(held.shape, jnp.flo...  12.2 us
    ppermute x3, starting transfers between devices, arrivals(): lax.ppermute(x, 'sub', [((i + shift) % p.subs, i) for i in range(p.subs)])  12.1 us
    pallas_call x1, Pallas kernels, inverse_call(): pl.pallas_call(kernel, out_shape=(square_shape, pltpu.VMEM(current.shape,...  8.37 us
    ppermute x4, starting transfers between devices, planned(): far.append(lax.ppermute(x, 'tri', swap))  7.37 us
  transfers between devices with their start and end apart: 36, of which 15 were waited for; matrix products, arithmetic and copies ran while one was open for 0% of the time, Pallas kernels for 13%

profile of v1, /device:TPU:1, one launch (start us, length us, event | category | flops | bytes accessed | tf_op | source)
XLA Modules:
  0.0 175.8 jit_solution(14624517898479426343)
XLA Ops:
  0.0 0.7 copy-done.2
  0.7 3.1 %extract.2 = bf16[8,4,32,512]{3,2,1,0:T(8,128)(2,1)} custom-call(s32[16]{0:T(128)S(1)} %copy-done.2, f32[36,256,512]{2,1,0:T(8,128)} %bitcast.2), custom_call_target="tpu_custom_call" | custom-call | tf_op jit(solution)/shard_map/extract/pallas_call | solution.py:277
  3.8 5.3 %all-to-all-start = ((bf16[8,4,32,512]{3,2,1,0:T(8,128)(2,1)}), bf16[8,4,32,512]{3,2,1,0:T(8,128)(2,1)S(1)}, u32[]{:S(2)}, u32[]{:S(2)}) async-start(bf16[8,4,32,512]{3,2,1,0:T(8,128)(2,1)} %extract.2), calls=%async_computation | async-start | bytes 2097152 | tf_op jit(solution)/shard_map/all_to_all | solution.py:678
  9.1 1.3 table.1.t
  10.4 12.5 %all-to-all-done.refs_0_ = bf16[8,4,32,512]{3,2,1,0:T(8,128)(2,1)S(1)} async-done(((bf16[8,4,32,512]{3,2,1,0:T(8,128)(2,1)}), bf16[8,4,32,512]{3,2,1,0:T(8,128)(2,1)S(1)}, u32[]{:S(2)}, u32[]{:S(2)}) %all-to-all-start) | async-done | bytes 1048608 | tf_op jit(solution)/shard_map/all_to_all | solution.py:678
  23.0 0.7 copy-done
  23.6 0.6 pick.2
  24.2 2.4 %collective-permute-start = (bf16[4,2,32,512]{3,2,1,0:T(8,128)(2,1)S(1)}, bf16[4,2,32,512]{3,2,1,0:T(8,128)(2,1)S(1)}, u32[]{:S(2)}, u32[]{:S(2)}) collective-permute-start(bf16[4,2,32,512]{3,2,1,0:T(8,128)(2,1)S(1)} %get-tuple-element.43.refs_0_), channel_id=1, source_target_pairs={{0,16},{2,18},{4,20},{6,22},{8,24},{10,26},{12,28},{14,30},{16,0},... | collective-permute-start | bytes 786440 | tf_op jit(solution)/shard_map/ppermute | solution.py:691
  26.6 10.4 %collective-permute-done.refs_1_ = bf16[4,2,32,512]{3,2,1,0:T(8,128)(2,1)S(1)} collective-permute-done((bf16[4,2,32,512]{3,2,1,0:T(8,128)(2,1)S(1)}, bf16[4,2,32,512]{3,2,1,0:T(8,128)(2,1)S(1)}, u32[]{:S(2)}, u32[]{:S(2)}) %collective-permute-start) | collective-permute-done | bytes 262176 | tf_op jit(solution)/shard_map/ppermute | solution.py:691
  37.0 1.0 build.3
  38.0 2.5 %collective-permute-start.1 = (bf16[4,32,512]{2,1,0:T(8,128)(2,1)S(1)}, bf16[4,32,512]{2,1,0:T(8,128)(2,1)S(1)}, u32[]{:S(2)}, u32[]{:S(2)}) collective-permute-start(bf16[4,32,512]{2,1,0:T(8,128)(2,1)S(1)} %get-tuple-element.45), channel_id=1, source_target_pairs={{0,2},{2,0},{4,6},{6,4},{8,10},{10,8},{12,14},{14,12},{16,18},{18,... | collective-permute-start | bytes 393224 | tf_op jit(solution)/shard_map/ppermute | solution.py:662
  40.6 1.3 collective-permute-start.3
  41.8 1.3 collective-permute-start.4
  43.1 1.3 collective-permute-start.5
  44.4 1.1 collective-permute-start.6
  45.5 1.1 collective-permute-start.7
  46.6 2.1 %extract.3 = (bf16[4,32,512]{2,1,0:T(8,128)(2,1)S(1)}, bf16[4,32,512]{2,1,0:T(8,128)(2,1)S(1)}, bf16[4,32,512]{2,1,0:T(8,128)(2,1)S(1)}, bf16[4,32,512]{2,1,0:T(...) custom-call(s32[16]{0:T(128)S(1)} %copy-done.3, ...), custom_call_target="tpu_custom_call" | custom-call | tf_op jit(solution)/shard_map/extract/pallas_call | solution.py:277
  48.8 1.4 collective-permute-start.9
  50.2 2.9 %collective-permute-start.10 = (bf16[4,32,512]{2,1,0:T(8,128)(2,1)S(1)}, bf16[4,32,512]{2,1,0:T(8,128)(2,1)S(1)}, u32[]{:S(2)}, u32[]{:S(2)}) collective-permute-start(bf16[4,32,512]{2,1,0:T(8,128)(2,1)S(1)} %get-tuple-element.57), channel_id=1, source_target_pairs={{0,4},{2,6},{4,0},{6,2},{8,12},{10,14},{12,8},{14,10},{16,20},{18,... | collective-permute-start | bytes 393224 | tf_op jit(solution)/shard_map/ppermute | solution.py:662
  53.1 0.5 collective-permute-done.7.refs_7_
  53.6 0.6 pack.3.refs_0_
  54.2 3.7 %collective-permute-start.8 = (bf16[8,4,32,512]{3,2,1,0:T(8,128)(2,1)S(1)}, bf16[8,4,32,512]{3,2,1,0:T(8,128)(2,1)S(1)}, u32[]{:S(2)}, u32[]{:S(2)}) collective-permute-start(bf16[8,4,32,512]{3,2,1,0:T(8,128)(2,1)S(1)} %pack.3.refs_0_), channel_id=1, source_target_pairs={{1,0},{0,1},{3,2},{2,3},{5,4},{4,5},{7,6},{6,7},{9,8},{8,9},{11,10... | collective-permute-start | bytes 3145736 | tf_op jit(solution)/shard_map/ppermute | solution.py:667
  57.9 1.1 collective-permute-start.12
  59.0 1.1 collective-permute-start.13
  60.1 1.6 collective-permute-start.14
  61.7 3.6 %collective-permute-start.15 = (bf16[4,32,512]{2,1,0:T(8,128)(2,1)S(1)}, bf16[4,32,512]{2,1,0:T(8,128)(2,1)S(1)}, u32[]{:S(2)}, u32[]{:S(2)}) collective-permute-start(bf16[4,32,512]{2,1,0:T(8,128)(2,1)S(1)} %get-tuple-element.62), channel_id=1, source_target_pairs={{0,14},{2,12},{4,10},{6,8},{8,6},{10,4},{12,2},{14,0},{16,30},{18,... | collective-permute-start | bytes 393224 | tf_op jit(solution)/shard_map/ppermute | solution.py:662
  65.3 1.1 collective-permute-done.13.refs_5_
  66.4 3.3 %collective-permute-done.14.refs_6_ = bf16[4,32,512]{2,1,0:T(8,128)(2,1)S(1)} collective-permute-done((bf16[4,32,512]{2,1,0:T(8,128)(2,1)S(1)}, bf16[4,32,512]{2,1,0:T(8,128)(2,1)S(1)}, u32[]{:S(2)}, u32[]{:S(2)}) %collective-permute-start.14) | collective-permute-done | bytes 131104 | tf_op jit(solution)/shard_map/ppermute | solution.py:662
  69.7 3.8 %collective-permute-done.15.refs_7_ = bf16[4,32,512]{2,1,0:T(8,128)(2,1)S(1)} collective-permute-done((bf16[4,32,512]{2,1,0:T(8,128)(2,1)S(1)}, bf16[4,32,512]{2,1,0:T(8,128)(2,1)S(1)}, u32[]{:S(2)}, u32[]{:S(2)}) %collective-permute-start.15) | collective-permute-done | bytes 131104 | tf_op jit(solution)/shard_map/ppermute | solution.py:662
  73.5 1.1 pick.3
  74.6 2.6 %collective-permute-start.26 = (bf16[4,2,32,512]{3,2,1,0:T(8,128)(2,1)S(1)}, bf16[4,2,32,512]{3,2,1,0:T(8,128)(2,1)S(1)}, u32[]{:S(2)}, u32[]{:S(2)}) collective-permute-start(bf16[4,2,32,512]{3,2,1,0:T(8,128)(2,1)S(1)} %get-tuple-element.72.refs_0_), channel_id=1, source_target_pairs={{0,16},{2,18},{4,20},{6,22},{8,24},{10,26},{12,28},{14,30},{16,0},... | collective-permute-start | bytes 786440 | tf_op jit(solution)/shard_map/ppermute | solution.py:691
  77.2 0.1 collective-permute-start.17
  77.3 2.3 %collective-permute-start.16 = (bf16[4,2,32,512]{3,2,1,0:T(8,128)(2,1)S(1)}, bf16[4,2,32,512]{3,2,1,0:T(8,128)(2,1)S(1)}, u32[]{:S(2)}, u32[]{:S(2)}) collective-permute-start(bf16[4,2,32,512]{3,2,1,0:T(8,128)(2,1)S(1)} %get-tuple-element.54.refs_0_), channel_id=1, source_target_pairs={{0,16},{2,18},{4,20},{6,22},{8,24},{10,26},{12,28},{14,30},{16,0},... | collective-permute-start | bytes 786440 | tf_op jit(solution)/shard_map/ppermute | solution.py:691
  79.6 21.0 %collective-permute-done.26.refs_1_ = bf16[4,2,32,512]{3,2,1,0:T(8,128)(2,1)S(1)} collective-permute-done((bf16[4,2,32,512]{3,2,1,0:T(8,128)(2,1)S(1)}, bf16[4,2,32,512]{3,2,1,0:T(8,128)(2,1)S(1)}, u32[]{:S(2)}, u32[]{:S(2)}) %collective-permute-start.26) | collective-permute-done | bytes 262176 | tf_op jit(solution)/shard_map/ppermute | solution.py:691
  100.6 0.9 build.5
  101.5 0.1 collective-permute-start.27
  101.5 0.1 collective-permute-start.28
  101.6 4.6 %collective-permute-done.17.refs_3_ = bf16[4,2,32,512]{3,2,1,0:T(8,128)(2,1)S(1)} collective-permute-done((bf16[4,2,32,512]{3,2,1,0:T(8,128)(2,1)S(1)}, bf16[4,2,32,512]{3,2,1,0:T(8,128)(2,1)S(1)}, u32[]{:S(2)}, u32[]{:S(2)}) %collective-permute-start.17) | collective-permute-done | bytes 262176 | tf_op jit(solution)/shard_map/ppermute | solution.py:691
  106.2 5.6 %collective-permute-done.16.refs_2_ = bf16[4,2,32,512]{3,2,1,0:T(8,128)(2,1)S(1)} collective-permute-done((bf16[4,2,32,512]{3,2,1,0:T(8,128)(2,1)S(1)}, bf16[4,2,32,512]{3,2,1,0:T(8,128)(2,1)S(1)}, u32[]{:S(2)}, u32[]{:S(2)}) %collective-permute-start.16) | collective-permute-done | bytes 262176 | tf_op jit(solution)/shard_map/ppermute | solution.py:691
  111.8 1.2 build.4
  113.0 0.1 collective-permute-start.18
  113.1 0.1 collective-permute-start.19
  113.2 2.5 %collective-permute-start.20 = (bf16[6,32,512]{2,1,0:T(8,128)(2,1)S(1)}, bf16[6,32,512]{2,1,0:T(8,128)(2,1)S(1)}, u32[]{:S(2)}, u32[]{:S(2)}) collective-permute-start(bf16[6,32,512]{2,1,0:T(8,128)(2,1)S(1)} %get-tuple-element.67), channel_id=1, source_target_pairs={{0,6},{2,4},{4,2},{6,0},{8,14},{10,12},{12,10},{14,8},{16,22},{18,... | collective-permute-start | bytes 589832 | tf_op jit(solution)/shard_map/ppermute | solution.py:662
  115.7 0.1 collective-permute-start.29
  115.8 8.7 %collective-permute-done.29.refs_3_ = bf16[3,32,512]{2,1,0:T(8,128)(2,1)S(1)} collective-permute-done((bf16[3,32,512]{2,1,0:T(8,128)(2,1)S(1)}, bf16[3,32,512]{2,1,0:T(8,128)(2,1)S(1)}, u32[]{:S(2)}, u32[]{:S(2)}) %collective-permute-start.29) | collective-permute-done | bytes 98336 | tf_op jit(solution)/shard_map/ppermute | solution.py:662
  124.5 0.2 collective-permute-start.21
  124.7 1.3 collective-permute-start.22
  126.1 2.4 %collective-permute-start.23 = (bf16[6,32,512]{2,1,0:T(8,128)(2,1)S(1)}, bf16[6,32,512]{2,1,0:T(8,128)(2,1)S(1)}, u32[]{:S(2)}, u32[]{:S(2)}) collective-permute-start(bf16[6,32,512]{2,1,0:T(8,128)(2,1)S(1)} %get-tuple-element.70), channel_id=1, source_target_pairs={{0,12},{2,14},{4,8},{6,10},{8,4},{10,6},{12,0},{14,2},{16,28},{18,... | collective-permute-start | bytes 589832 | tf_op jit(solution)/shard_map/ppermute | solution.py:662
  128.4 0.8 collective-permute-start.24
  129.3 0.6 collective-permute-start.30
  129.9 4.0 %collective-permute-done.22.refs_5_ = bf16[6,32,512]{2,1,0:T(8,128)(2,1)S(1)} collective-permute-done((bf16[6,32,512]{2,1,0:T(8,128)(2,1)S(1)}, bf16[6,32,512]{2,1,0:T(8,128)(2,1)S(1)}, u32[]{:S(2)}, u32[]{:S(2)}) %collective-permute-start.22) | collective-permute-done | bytes 196640 | tf_op jit(solution)/shard_map/ppermute | solution.py:662
  133.9 0.9 collective-permute-start.31
  134.7 4.5 %collective-permute-done.23.refs_6_ = bf16[6,32,512]{2,1,0:T(8,128)(2,1)S(1)} collective-permute-done((bf16[6,32,512]{2,1,0:T(8,128)(2,1)S(1)}, bf16[6,32,512]{2,1,0:T(8,128)(2,1)S(1)}, u32[]{:S(2)}, u32[]{:S(2)}) %collective-permute-start.23) | collective-permute-done | bytes 196640 | tf_op jit(solution)/shard_map/ppermute | solution.py:662
  139.2 3.2 %collective-permute-done.24.refs_7_ = bf16[6,32,512]{2,1,0:T(8,128)(2,1)S(1)} collective-permute-done((bf16[6,32,512]{2,1,0:T(8,128)(2,1)S(1)}, bf16[6,32,512]{2,1,0:T(8,128)(2,1)S(1)}, u32[]{:S(2)}, u32[]{:S(2)}) %collective-permute-start.24) | collective-permute-done | bytes 196640 | tf_op jit(solution)/shard_map/ppermute | solution.py:662
  142.4 1.7 collective-permute-start.33
  144.1 0.6 pack.4.refs_2_
  144.7 4.8 %collective-permute-start.25 = (bf16[8,6,32,512]{3,2,1,0:T(8,128)(2,1)S(1)}, bf16[8,6,32,512]{3,2,1,0:T(8,128)(2,1)S(1)}, u32[]{:S(2)}, u32[]{:S(2)}) collective-permute-start(bf16[8,6,32,512]{3,2,1,0:T(8,128)(2,1)S(1)} %pack.4.refs_2_), channel_id=1, source_target_pairs={{1,0},{0,1},{3,2},{2,3},{5,4},{4,5},{7,6},{6,7},{9,8},{8,9},{11,10... | collective-permute-start | bytes 4718600 | tf_op jit(solution)/shard_map/ppermute | solution.py:667
  149.5 0.3 collective-permute-done.32.refs_6_
  149.8 1.0 collective-permute-done.33.refs_7_
  150.8 0.6 pack.5.refs_4_
  151.4 3.6 %collective-permute-start.34 = (bf16[8,3,32,512]{3,2,1,0:T(8,128)(2,1)S(1)}, bf16[8,3,32,512]{3,2,1,0:T(8,128)(2,1)S(1)}, u32[]{:S(2)}, u32[]{:S(2)}) collective-permute-start(bf16[8,3,32,512]{3,2,1,0:T(8,128)(2,1)S(1)} %pack.5.refs_4_), channel_id=1, source_target_pairs={{1,0},{0,1},{3,2},{2,3},{5,4},{4,5},{7,6},{6,7},{9,8},{8,9},{11,10... | collective-permute-start | bytes 2359304 | tf_op jit(solution)/shard_map/ppermute | solution.py:667
  155.0 8.4 %inverse.1 = (bf16[512,512]{1,0:T(8,128)(2,1)S(1)}, f32[36,256,512]{2,1,0:T(8,128)S(1)}) custom-call(s32[40]{0:T(128)S(1)} %copy-done.1, bf16[8,4,32,512]{3,2,1,0:T(8,128)(2,1)S(1)} %pack.3.refs_0_, bf16[8,4,32,512]{3,2,1,0:T(8,128)(2,1)S(1)} %collective-permute-done.8.refs_1_, f32[36,256,512]{2,1,0:T(8,128)} %bitcast.4), custom_call_target="tpu_custom_call" | custom-call | flops 16106127360 | bytes 1048576 | tf_op jit(solution)/shard_map/inverse/pallas_call | solution.py:478
  163.4 6.5 %begin.1.refs_6_ = f32[36,256,512]{2,1,0:T(8,128)} custom-call(s32[40]{0:T(128)S(1)} %copy-done.1, f32[36,256,512]{2,1,0:T(8,128)S(1)} %get-tuple-element.52.tiles, bf16[512,512]{1,0:T(8,128)(2,1)S(1)} %get-tuple-element.53.inv, bf16[8,4,32,512]{3,2,1,0:T(8,128)(2,1)S(1)} %pack.3.refs_0_, bf16[8,4,32,512]{3,2,1,0:T(8,128)(2,1)S(1)} %collective-permute-done.8.refs_1_, ...), custom_call_target="tpu_custom_call" | custom-call | tf_op jit(solution)/shard_map/begin/pallas_call | solution.py:626
  169.9 5.6 %finish.1 = f32[36,256,512]{2,1,0:T(8,128)} custom-call(s32[40]{0:T(128)S(1)} %copy-done.1, f32[36,256,512]{2,1,0:T(8,128)S(1)} %get-tuple-element.52.tiles, bf16[512,512]{1,0:T(8,128)(2,1)S(1)} %get-tuple-element.53.inv, bf16[8,4,32,512]{3,2,1,0:T(8,128)(2,1)S(1)} %pack.3.refs_0_, ...), custom_call_target="tpu_custom_call", output_to_operand_aliasing={{}: (9, {})} | custom-call | tf_op jit(solution)/shard_map/finish/pallas_call | solution.py:626
  (30 shorter events, 0.1 us)
Async XLA Ops:
  0.0 46.6 %copy-start.3 = (s32[16]{0:T(128)S(1)}, s32[16]{0:T(128)}, u32[]{:S(2)}) copy-start(s32[16]{0:T(128)} %owner.5) | copy-start | bytes 196
  0.0 0.7 copy-start.2
  3.8 19.1 %all-to-all-start = ((bf16[8,4,32,512]{3,2,1,0:T(8,128)(2,1)}), bf16[8,4,32,512]{3,2,1,0:T(8,128)(2,1)S(1)}, u32[]{:S(2)}, u32[]{:S(2)}) async-start(bf16[8,4,32,512]{3,2,1,0:T(8,128)(2,1)} %extract.2), calls=%async_computation | async-start | bytes 2097152 | tf_op jit(solution)/shard_map/all_to_all | solution.py:678
  23.0 0.7 copy-start
  23.6 30.0 %copy-start.1 = (s32[40]{0:T(128)S(1)}, s32[40]{0:T(128)}, u32[]{:S(2)}) copy-start(s32[40]{0:T(128)} %table.1.t) | copy-start | bytes 484
  24.2 12.8 %collective-permute-start = (bf16[4,2,32,512]{3,2,1,0:T(8,128)(2,1)S(1)}, bf16[4,2,32,512]{3,2,1,0:T(8,128)(2,1)S(1)}, u32[]{:S(2)}, u32[]{:S(2)}) collective-permute-start(bf16[4,2,32,512]{3,2,1,0:T(8,128)(2,1)S(1)} %get-tuple-element.43.refs_0_), channel_id=1, source_target_pairs={{0,16},{2,18},{4,20},{6,22},{8,24},{10,26},{12,28},{14,30},{16,0},... | collective-permute-start | bytes 786440 | tf_op jit(solution)/shard_map/ppermute | solution.py:691
  38.0 6.4 %collective-permute-start.1 = (bf16[4,32,512]{2,1,0:T(8,128)(2,1)S(1)}, bf16[4,32,512]{2,1,0:T(8,128)(2,1)S(1)}, u32[]{:S(2)}, u32[]{:S(2)}) collective-permute-start(bf16[4,32,512]{2,1,0:T(8,128)(2,1)S(1)} %get-tuple-element.45), channel_id=1, source_target_pairs={{0,2},{2,0},{4,6},{6,4},{8,10},{10,8},{12,14},{14,12},{16,18},{18,... | collective-permute-start | bytes 393224 | tf_op jit(solution)/shard_map/ppermute | solution.py:662
  40.6 4.9 %collective-permute-start.2 = (bf16[4,32,512]{2,1,0:T(8,128)(2,1)S(1)}, bf16[4,32,512]{2,1,0:T(8,128)(2,1)S(1)}, u32[]{:S(2)}, u32[]{:S(2)}) collective-permute-start(bf16[4,32,512]{2,1,0:T(8,128)(2,1)S(1)} %get-tuple-element.46), channel_id=1, source_target_pairs={{0,4},{2,6},{4,0},{6,2},{8,12},{10,14},{12,8},{14,10},{16,20},{18,... | collective-permute-start | bytes 393224 | tf_op jit(solution)/shard_map/ppermute | solution.py:662
  40.6 8.2 %collective-permute-start.3 = (bf16[4,32,512]{2,1,0:T(8,128)(2,1)S(1)}, bf16[4,32,512]{2,1,0:T(8,128)(2,1)S(1)}, u32[]{:S(2)}, u32[]{:S(2)}) collective-permute-start(bf16[4,32,512]{2,1,0:T(8,128)(2,1)S(1)} %get-tuple-element.47), channel_id=1, source_target_pairs={{0,6},{2,4},{4,2},{6,0},{8,14},{10,12},{12,10},{14,8},{16,22},{18,... | collective-permute-start | bytes 393224 | tf_op jit(solution)/shard_map/ppermute | solution.py:662
  41.8 8.4 %collective-permute-start.4 = (bf16[4,32,512]{2,1,0:T(8,128)(2,1)S(1)}, bf16[4,32,512]{2,1,0:T(8,128)(2,1)S(1)}, u32[]{:S(2)}, u32[]{:S(2)}) collective-permute-start(bf16[4,32,512]{2,1,0:T(8,128)(2,1)S(1)} %get-tuple-element.48), channel_id=1, source_target_pairs={{0,8},{2,10},{4,12},{6,14},{8,0},{10,2},{12,4},{14,6},{16,24},{18,... | collective-permute-start | bytes 393224 | tf_op jit(solution)/shard_map/ppermute | solution.py:662
  43.1 9.9 %collective-permute-start.5 = (bf16[4,32,512]{2,1,0:T(8,128)(2,1)S(1)}, bf16[4,32,512]{2,1,0:T(8,128)(2,1)S(1)}, u32[]{:S(2)}, u32[]{:S(2)}) collective-permute-start(bf16[4,32,512]{2,1,0:T(8,128)(2,1)S(1)} %get-tuple-element.49), channel_id=1, source_target_pairs={{0,10},{2,8},{4,14},{6,12},{8,2},{10,0},{12,6},{14,4},{16,26},{18,... | collective-permute-start | bytes 393224 | tf_op jit(solution)/shard_map/ppermute | solution.py:662
  44.4 8.7 %collective-permute-start.6 = (bf16[4,32,512]{2,1,0:T(8,128)(2,1)S(1)}, bf16[4,32,512]{2,1,0:T(8,128)(2,1)S(1)}, u32[]{:S(2)}, u32[]{:S(2)}) collective-permute-start(bf16[4,32,512]{2,1,0:T(8,128)(2,1)S(1)} %get-tuple-element.50), channel_id=1, source_target_pairs={{0,12},{2,14},{4,8},{6,10},{8,4},{10,6},{12,0},{14,2},{16,28},{18,... | collective-permute-start | bytes 393224 | tf_op jit(solution)/shard_map/ppermute | solution.py:662
  45.5 8.1 %collective-permute-start.7 = (bf16[4,32,512]{2,1,0:T(8,128)(2,1)S(1)}, bf16[4,32,512]{2,1,0:T(8,128)(2,1)S(1)}, u32[]{:S(2)}, u32[]{:S(2)}) collective-permute-start(bf16[4,32,512]{2,1,0:T(8,128)(2,1)S(1)} %get-tuple-element.51), channel_id=1, source_target_pairs={{0,14},{2,12},{4,10},{6,8},{8,6},{10,4},{12,2},{14,0},{16,30},{18,... | collective-permute-start | bytes 393224 | tf_op jit(solution)/shard_map/ppermute | solution.py:662
  48.8 10.3 %collective-permute-start.9 = (bf16[4,32,512]{2,1,0:T(8,128)(2,1)S(1)}, bf16[4,32,512]{2,1,0:T(8,128)(2,1)S(1)}, u32[]{:S(2)}, u32[]{:S(2)}) collective-permute-start(bf16[4,32,512]{2,1,0:T(8,128)(2,1)S(1)} %get-tuple-element.56), channel_id=1, source_target_pairs={{0,2},{2,0},{4,6},{6,4},{8,10},{10,8},{12,14},{14,12},{16,18},{18,... | collective-permute-start | bytes 393224 | tf_op jit(solution)/shard_map/ppermute | solution.py:662
  50.2 9.9 %collective-permute-start.10 = (bf16[4,32,512]{2,1,0:T(8,128)(2,1)S(1)}, bf16[4,32,512]{2,1,0:T(8,128)(2,1)S(1)}, u32[]{:S(2)}, u32[]{:S(2)}) collective-permute-start(bf16[4,32,512]{2,1,0:T(8,128)(2,1)S(1)} %get-tuple-element.57), channel_id=1, source_target_pairs={{0,4},{2,6},{4,0},{6,2},{8,12},{10,14},{12,8},{14,10},{16,20},{18,... | collective-permute-start | bytes 393224 | tf_op jit(solution)/shard_map/ppermute | solution.py:662
  53.1 8.6 %collective-permute-start.11 = (bf16[4,32,512]{2,1,0:T(8,128)(2,1)S(1)}, bf16[4,32,512]{2,1,0:T(8,128)(2,1)S(1)}, u32[]{:S(2)}, u32[]{:S(2)}) collective-permute-start(bf16[4,32,512]{2,1,0:T(8,128)(2,1)S(1)} %get-tuple-element.58), channel_id=1, source_target_pairs={{0,6},{2,4},{4,2},{6,0},{8,14},{10,12},{12,10},{14,8},{16,22},{18,... | collective-permute-start | bytes 393224 | tf_op jit(solution)/shard_map/ppermute | solution.py:662
  54.2 100.8 %collective-permute-start.8 = (bf16[8,4,32,512]{3,2,1,0:T(8,128)(2,1)S(1)}, bf16[8,4,32,512]{3,2,1,0:T(8,128)(2,1)S(1)}, u32[]{:S(2)}, u32[]{:S(2)}) collective-permute-start(bf16[8,4,32,512]{3,2,1,0:T(8,128)(2,1)S(1)} %pack.3.refs_0_), channel_id=1, source_target_pairs={{1,0},{0,1},{3,2},{2,3},{5,4},{4,5},{7,6},{6,7},{9,8},{8,9},{11,10... | collective-permute-start | bytes 3145736 | tf_op jit(solution)/shard_map/ppermute | solution.py:667
  57.9 7.4 %collective-permute-start.12 = (bf16[4,32,512]{2,1,0:T(8,128)(2,1)S(1)}, bf16[4,32,512]{2,1,0:T(8,128)(2,1)S(1)}, u32[]{:S(2)}, u32[]{:S(2)}) collective-permute-start(bf16[4,32,512]{2,1,0:T(8,128)(2,1)S(1)} %get-tuple-element.59), channel_id=1, source_target_pairs={{0,8},{2,10},{4,12},{6,14},{8,0},{10,2},{12,4},{14,6},{16,24},{18,... | collective-permute-start | bytes 393224 | tf_op jit(solution)/shard_map/ppermute | solution.py:662
  59.0 7.4 %collective-permute-start.13 = (bf16[4,32,512]{2,1,0:T(8,128)(2,1)S(1)}, bf16[4,32,512]{2,1,0:T(8,128)(2,1)S(1)}, u32[]{:S(2)}, u32[]{:S(2)}) collective-permute-start(bf16[4,32,512]{2,1,0:T(8,128)(2,1)S(1)} %get-tuple-element.60), channel_id=1, source_target_pairs={{0,10},{2,8},{4,14},{6,12},{8,2},{10,0},{12,6},{14,4},{16,26},{18,... | collective-permute-start | bytes 393224 | tf_op jit(solution)/shard_map/ppermute | solution.py:662
  60.1 9.6 %collective-permute-start.14 = (bf16[4,32,512]{2,1,0:T(8,128)(2,1)S(1)}, bf16[4,32,512]{2,1,0:T(8,128)(2,1)S(1)}, u32[]{:S(2)}, u32[]{:S(2)}) collective-permute-start(bf16[4,32,512]{2,1,0:T(8,128)(2,1)S(1)} %get-tuple-element.61), channel_id=1, source_target_pairs={{0,12},{2,14},{4,8},{6,10},{8,4},{10,6},{12,0},{14,2},{16,28},{18,... | collective-permute-start | bytes 393224 | tf_op jit(solution)/shard_map/ppermute | solution.py:662
  61.7 11.8 %collective-permute-start.15 = (bf16[4,32,512]{2,1,0:T(8,128)(2,1)S(1)}, bf16[4,32,512]{2,1,0:T(8,128)(2,1)S(1)}, u32[]{:S(2)}, u32[]{:S(2)}) collective-permute-start(bf16[4,32,512]{2,1,0:T(8,128)(2,1)S(1)} %get-tuple-element.62), channel_id=1, source_target_pairs={{0,14},{2,12},{4,10},{6,8},{8,6},{10,4},{12,2},{14,0},{16,30},{18,... | collective-permute-start | bytes 393224 | tf_op jit(solution)/shard_map/ppermute | solution.py:662
  74.6 26.0 %collective-permute-start.26 = (bf16[4,2,32,512]{3,2,1,0:T(8,128)(2,1)S(1)}, bf16[4,2,32,512]{3,2,1,0:T(8,128)(2,1)S(1)}, u32[]{:S(2)}, u32[]{:S(2)}) collective-permute-start(bf16[4,2,32,512]{3,2,1,0:T(8,128)(2,1)S(1)} %get-tuple-element.72.refs_0_), channel_id=1, source_target_pairs={{0,16},{2,18},{4,20},{6,22},{8,24},{10,26},{12,28},{14,30},{16,0},... | collective-permute-start | bytes 786440 | tf_op jit(solution)/shard_map/ppermute | solution.py:691
  77.2 29.0 %collective-permute-start.17 = (bf16[4,2,32,512]{3,2,1,0:T(8,128)(2,1)S(1)}, bf16[4,2,32,512]{3,2,1,0:T(8,128)(2,1)S(1)}, u32[]{:S(2)}, u32[]{:S(2)}) collective-permute-start(bf16[4,2,32,512]{3,2,1,0:T(8,128)(2,1)S(1)} %get-tuple-element.63.refs_1_), channel_id=1, source_target_pairs={{0,16},{2,18},{4,20},{6,22},{8,24},{10,26},{12,28},{14,30},{16,0},... | collective-permute-start | bytes 786440 | tf_op jit(solution)/shard_map/ppermute | solution.py:691
  77.3 34.5 %collective-permute-start.16 = (bf16[4,2,32,512]{3,2,1,0:T(8,128)(2,1)S(1)}, bf16[4,2,32,512]{3,2,1,0:T(8,128)(2,1)S(1)}, u32[]{:S(2)}, u32[]{:S(2)}) collective-permute-start(bf16[4,2,32,512]{3,2,1,0:T(8,128)(2,1)S(1)} %get-tuple-element.54.refs_0_), channel_id=1, source_target_pairs={{0,16},{2,18},{4,20},{6,22},{8,24},{10,26},{12,28},{14,30},{16,0},... | collective-permute-start | bytes 786440 | tf_op jit(solution)/shard_map/ppermute | solution.py:691
  101.5 11.7 %collective-permute-start.27 = (bf16[3,32,512]{2,1,0:T(8,128)(2,1)S(1)}, bf16[3,32,512]{2,1,0:T(8,128)(2,1)S(1)}, u32[]{:S(2)}, u32[]{:S(2)}) collective-permute-start(bf16[3,32,512]{2,1,0:T(8,128)(2,1)S(1)} %get-tuple-element.74), channel_id=1, source_target_pairs={{0,2},{2,0},{4,6},{6,4},{8,10},{10,8},{12,14},{14,12},{16,18},{18,... | collective-permute-start | bytes 294920 | tf_op jit(solution)/shard_map/ppermute | solution.py:662
  101.5 14.2 %collective-permute-start.28 = (bf16[3,32,512]{2,1,0:T(8,128)(2,1)S(1)}, bf16[3,32,512]{2,1,0:T(8,128)(2,1)S(1)}, u32[]{:S(2)}, u32[]{:S(2)}) collective-permute-start(bf16[3,32,512]{2,1,0:T(8,128)(2,1)S(1)} %get-tuple-element.75), channel_id=1, source_target_pairs={{0,4},{2,6},{4,0},{6,2},{8,12},{10,14},{12,8},{14,10},{16,20},{18,... | collective-permute-start | bytes 294920 | tf_op jit(solution)/shard_map/ppermute | solution.py:662
  113.0 11.7 %collective-permute-start.18 = (bf16[6,32,512]{2,1,0:T(8,128)(2,1)S(1)}, bf16[6,32,512]{2,1,0:T(8,128)(2,1)S(1)}, u32[]{:S(2)}, u32[]{:S(2)}) collective-permute-start(bf16[6,32,512]{2,1,0:T(8,128)(2,1)S(1)} %get-tuple-element.65), channel_id=1, source_target_pairs={{0,2},{2,0},{4,6},{6,4},{8,10},{10,8},{12,14},{14,12},{16,18},{18,... | collective-permute-start | bytes 589832 | tf_op jit(solution)/shard_map/ppermute | solution.py:662
  113.1 13.0 %collective-permute-start.19 = (bf16[6,32,512]{2,1,0:T(8,128)(2,1)S(1)}, bf16[6,32,512]{2,1,0:T(8,128)(2,1)S(1)}, u32[]{:S(2)}, u32[]{:S(2)}) collective-permute-start(bf16[6,32,512]{2,1,0:T(8,128)(2,1)S(1)} %get-tuple-element.66), channel_id=1, source_target_pairs={{0,4},{2,6},{4,0},{6,2},{8,12},{10,14},{12,8},{14,10},{16,20},{18,... | collective-permute-start | bytes 589832 | tf_op jit(solution)/shard_map/ppermute | solution.py:662
  113.2 15.3 %collective-permute-start.20 = (bf16[6,32,512]{2,1,0:T(8,128)(2,1)S(1)}, bf16[6,32,512]{2,1,0:T(8,128)(2,1)S(1)}, u32[]{:S(2)}, u32[]{:S(2)}) collective-permute-start(bf16[6,32,512]{2,1,0:T(8,128)(2,1)S(1)} %get-tuple-element.67), channel_id=1, source_target_pairs={{0,6},{2,4},{4,2},{6,0},{8,14},{10,12},{12,10},{14,8},{16,22},{18,... | collective-permute-start | bytes 589832 | tf_op jit(solution)/shard_map/ppermute | solution.py:662
  115.7 8.8 %collective-permute-start.29 = (bf16[3,32,512]{2,1,0:T(8,128)(2,1)S(1)}, bf16[3,32,512]{2,1,0:T(8,128)(2,1)S(1)}, u32[]{:S(2)}, u32[]{:S(2)}) collective-permute-start(bf16[3,32,512]{2,1,0:T(8,128)(2,1)S(1)} %get-tuple-element.76), channel_id=1, source_target_pairs={{0,6},{2,4},{4,2},{6,0},{8,14},{10,12},{12,10},{14,8},{16,22},{18,... | collective-permute-start | bytes 294920 | tf_op jit(solution)/shard_map/ppermute | solution.py:662
  124.5 4.7 %collective-permute-start.21 = (bf16[6,32,512]{2,1,0:T(8,128)(2,1)S(1)}, bf16[6,32,512]{2,1,0:T(8,128)(2,1)S(1)}, u32[]{:S(2)}, u32[]{:S(2)}) collective-permute-start(bf16[6,32,512]{2,1,0:T(8,128)(2,1)S(1)} %get-tuple-element.68), channel_id=1, source_target_pairs={{0,8},{2,10},{4,12},{6,14},{8,0},{10,2},{12,4},{14,6},{16,24},{18,... | collective-permute-start | bytes 589832 | tf_op jit(solution)/shard_map/ppermute | solution.py:662
  124.7 9.1 %collective-permute-start.22 = (bf16[6,32,512]{2,1,0:T(8,128)(2,1)S(1)}, bf16[6,32,512]{2,1,0:T(8,128)(2,1)S(1)}, u32[]{:S(2)}, u32[]{:S(2)}) collective-permute-start(bf16[6,32,512]{2,1,0:T(8,128)(2,1)S(1)} %get-tuple-element.69), channel_id=1, source_target_pairs={{0,10},{2,8},{4,14},{6,12},{8,2},{10,0},{12,6},{14,4},{16,26},{18,... | collective-permute-start | bytes 589832 | tf_op jit(solution)/shard_map/ppermute | solution.py:662
  126.1 13.2 %collective-permute-start.23 = (bf16[6,32,512]{2,1,0:T(8,128)(2,1)S(1)}, bf16[6,32,512]{2,1,0:T(8,128)(2,1)S(1)}, u32[]{:S(2)}, u32[]{:S(2)}) collective-permute-start(bf16[6,32,512]{2,1,0:T(8,128)(2,1)S(1)} %get-tuple-element.70), channel_id=1, source_target_pairs={{0,12},{2,14},{4,8},{6,10},{8,4},{10,6},{12,0},{14,2},{16,28},{18,... | collective-permute-start | bytes 589832 | tf_op jit(solution)/shard_map/ppermute | solution.py:662
  128.4 14.0 %collective-permute-start.24 = (bf16[6,32,512]{2,1,0:T(8,128)(2,1)S(1)}, bf16[6,32,512]{2,1,0:T(8,128)(2,1)S(1)}, u32[]{:S(2)}, u32[]{:S(2)}) collective-permute-start(bf16[6,32,512]{2,1,0:T(8,128)(2,1)S(1)} %get-tuple-element.71), channel_id=1, source_target_pairs={{0,14},{2,12},{4,10},{6,8},{8,6},{10,4},{12,2},{14,0},{16,30},{18,... | collective-permute-start | bytes 589832 | tf_op jit(solution)/shard_map/ppermute | solution.py:662
  129.3 15.5 %collective-permute-start.30 = (bf16[3,32,512]{2,1,0:T(8,128)(2,1)S(1)}, bf16[3,32,512]{2,1,0:T(8,128)(2,1)S(1)}, u32[]{:S(2)}, u32[]{:S(2)}) collective-permute-start(bf16[3,32,512]{2,1,0:T(8,128)(2,1)S(1)} %get-tuple-element.77), channel_id=1, source_target_pairs={{0,8},{2,10},{4,12},{6,14},{8,0},{10,2},{12,4},{14,6},{16,24},{18,... | collective-permute-start | bytes 294920 | tf_op jit(solution)/shard_map/ppermute | solution.py:662
  133.9 15.7 %collective-permute-start.31 = (bf16[3,32,512]{2,1,0:T(8,128)(2,1)S(1)}, bf16[3,32,512]{2,1,0:T(8,128)(2,1)S(1)}, u32[]{:S(2)}, u32[]{:S(2)}) collective-permute-start(bf16[3,32,512]{2,1,0:T(8,128)(2,1)S(1)} %get-tuple-element.78), channel_id=1, source_target_pairs={{0,10},{2,8},{4,14},{6,12},{8,2},{10,0},{12,6},{14,4},{16,26},{18,... | collective-permute-start | bytes 294920 | tf_op jit(solution)/shard_map/ppermute | solution.py:662
  139.2 10.5 %collective-permute-start.32 = (bf16[3,32,512]{2,1,0:T(8,128)(2,1)S(1)}, bf16[3,32,512]{2,1,0:T(8,128)(2,1)S(1)}, u32[]{:S(2)}, u32[]{:S(2)}) collective-permute-start(bf16[3,32,512]{2,1,0:T(8,128)(2,1)S(1)} %get-tuple-element.79), channel_id=1, source_target_pairs={{0,12},{2,14},{4,8},{6,10},{8,4},{10,6},{12,0},{14,2},{16,28},{18,... | collective-permute-start | bytes 294920 | tf_op jit(solution)/shard_map/ppermute | solution.py:662
  142.4 8.4 %collective-permute-start.33 = (bf16[3,32,512]{2,1,0:T(8,128)(2,1)S(1)}, bf16[3,32,512]{2,1,0:T(8,128)(2,1)S(1)}, u32[]{:S(2)}, u32[]{:S(2)}) collective-permute-start(bf16[3,32,512]{2,1,0:T(8,128)(2,1)S(1)} %get-tuple-element.80), channel_id=1, source_target_pairs={{0,14},{2,12},{4,10},{6,8},{8,6},{10,4},{12,2},{14,0},{16,30},{18,... | collective-permute-start | bytes 294920 | tf_op jit(solution)/shard_map/ppermute | solution.py:662
  144.7 18.7 %collective-permute-start.25 = (bf16[8,6,32,512]{3,2,1,0:T(8,128)(2,1)S(1)}, bf16[8,6,32,512]{3,2,1,0:T(8,128)(2,1)S(1)}, u32[]{:S(2)}, u32[]{:S(2)}) collective-permute-start(bf16[8,6,32,512]{3,2,1,0:T(8,128)(2,1)S(1)} %pack.4.refs_2_), channel_id=1, source_target_pairs={{1,0},{0,1},{3,2},{2,3},{5,4},{4,5},{7,6},{6,7},{9,8},{8,9},{11,10... | collective-permute-start | bytes 4718600 | tf_op jit(solution)/shard_map/ppermute | solution.py:667
  151.4 18.5 %collective-permute-start.34 = (bf16[8,3,32,512]{3,2,1,0:T(8,128)(2,1)S(1)}, bf16[8,3,32,512]{3,2,1,0:T(8,128)(2,1)S(1)}, u32[]{:S(2)}, u32[]{:S(2)}) collective-permute-start(bf16[8,3,32,512]{3,2,1,0:T(8,128)(2,1)S(1)} %pack.5.refs_4_), channel_id=1, source_target_pairs={{1,0},{0,1},{3,2},{2,3},{5,4},{4,5},{7,6},{6,7},{9,8},{8,9},{11,10... | collective-permute-start | bytes 2359304 | tf_op jit(solution)/shard_map/ppermute | solution.py:667
